TPU v7x, 128 devices: a whole 4x4x4 slice. The times are simulated.
128 devices in a mesh: gx: 16 (over y, x_lo, core), gy: 8 (over z, x_hi).
Axes of the slice: x: 4 (x_hi: 2, x_lo: 2; x = x_hi * 2 + x_lo), y: 4, z: 4, core: 2. Of those that a mesh axis runs over, the one named last changes fastest.
Arguments:
- thinker_normed: bfloat16 [8, 16, 8192], P(None, None, 'gx'), may hold values from -6 to 6
- thinker_resid: bfloat16 [8, 16, 8192], P('gy', None, 'gx'), may hold values from -6 to 6
- gate_weight: bfloat16 [8192, 29568], P('gx', 'gy'), may hold values from -0.0625 to 0.0625
- up_weight: bfloat16 [8192, 29568], P('gx', 'gy'), may hold values from -0.0625 to 0.0625
- down_weight: bfloat16 [29568, 8192], P('gy', 'gx'), may hold values from -0.03125 to 0.03125
- bridge_weight: bfloat16 [8192, 3584], P('gx'), may hold values from -0.0625 to 0.0625
- talker_stream: bfloat16 [8, 3072, 3584], P('gy', 'gx'), may hold values from -6 to 6
- norm_gain: float32 [3584], replicated, may hold values from 0.5 to 2
- w_query: bfloat16 [3584, 1792], P(None, 'gy'), may hold values from -0.09375 to 0.09375
- w_key: bfloat16 [3584, 256], P(None, 'gy'), may hold values from -0.09375 to 0.09375
- w_value: bfloat16 [3584, 256], P(None, 'gy'), may hold values from -0.09375 to 0.09375
- a_query: bfloat16 [3584, 64], replicated, may hold values from -0.09375 to 0.09375
- b_query: bfloat16 [64, 1792], replicated, may hold values from -0.75 to 0.75
- a_value: bfloat16 [3584, 64], replicated, may hold values from -0.09375 to 0.09375
- b_value: bfloat16 [64, 256], replicated, may hold values from -0.75 to 0.75
- text_index: int32 [8, 3072], P('gy', 'gx'), may hold values from 0 to 15
- span_offset: int32 [8], P('gy'), may hold values from 1 to 3071
- out_grad: bfloat16 [8, 3072, 1792], P('gy', 'gx'), may hold values from -6 to 6
Outputs:
- attn_out: bfloat16 [8, 3072, 1792], P('gy', 'gx')
- grad_aq: float32 [3584, 64], replicated
- grad_bq: float32 [64, 1792], replicated
- grad_av: float32 [3584, 64], replicated
- grad_bv: float32 [64, 256], replicated
All inputs are finite; a program needn't handle non-finite values.
Results may differ from a plain program's by a relative error of at most 0.035.
Values may be sent and summed in bfloat16 or wider, within the bound.
A program may use at most 192 MiB of HBM per device.

v0:
```python
import math

import jax
import jax.numpy as jnp
from jax import lax
from jax.sharding import PartitionSpec as P

HEADS = 14
KVH = 2
HD = 128


rope_base = 1000000.0
norm_eps = 1e-06


def cut_along(array, dim, size):
    dims = array.shape
    parts = array.reshape(*dims[:dim], size, dims[dim] // size, *dims[dim + 1 :])
    return jnp.moveaxis(parts, dim, 0)


def sent_and_summed(array, axis, dim):
    size = lax.axis_size(axis)
    parts = lax.all_to_all(cut_along(array, dim, size), axis, 0, 0, tiled=True)
    return jnp.sum(parts, axis=0)


def angle_tables(first_pos, length):
    position = (first_pos + jnp.arange(length, dtype=jnp.int32)).astype(jnp.float32)
    frequency = rope_base ** (-(2.0 * jnp.arange(HD // 2, dtype=jnp.float32)) / HD)
    angles = position[:, None] * frequency[None, :]
    return (jnp.cos(angles), jnp.sin(angles))


def rotate(tensor, cosine, sine_table, signed):
    layout = (cosine.shape[0],) + (1,) * (tensor.ndim - 2) + (cosine.shape[1],)
    cosine = cosine.reshape(layout)
    sine_part = sine_table.reshape(layout) * signed
    half_width = tensor.shape[-1] // 2
    first_half = tensor[..., :half_width]
    second_half = tensor[..., half_width:]
    return jnp.concatenate(
        [
            first_half * cosine - second_half * sine_part,
            second_half * cosine + first_half * sine_part,
        ],
        axis=-1,
    )


def on_device(
    thinker_normed,
    thinker_resid,
    gate_weight,
    up_weight,
    down_weight,
    bridge_weight,
    talker_stream,
    norm_gain,
    w_query,
    w_key,
    w_value,
    a_query,
    b_query,
    a_value,
    b_value,
    text_index,
    span_offset,
    out_grad,
):
    seq_count, rows_seq, columns = thinker_normed.shape
    normed = thinker_normed.reshape(seq_count * rows_seq, columns)
    ff_local = gate_weight.shape[1]
    block = normed
    gate_part = jnp.dot(block, gate_weight, preferred_element_type=jnp.float32)
    up_part = jnp.dot(block, up_weight, preferred_element_type=jnp.float32)
    both_parts = sent_and_summed(jnp.concatenate([gate_part, up_part], axis=1), "gx", 0)
    hidden = (jax.nn.silu(both_parts[:, :ff_local]) * both_parts[:, ff_local:]).astype(jnp.bfloat16)
    partial_out = jnp.dot(
        lax.all_gather(hidden, "gx", axis=0, tiled=True),
        down_weight,
        preferred_element_type=jnp.float32,
    )
    summed = sent_and_summed(partial_out, "gy", 0)
    thinker_out = (summed + thinker_resid[0].astype(jnp.float32)).astype(jnp.bfloat16)
    bridge_part = jnp.dot(thinker_out, bridge_weight, preferred_element_type=jnp.float32)
    bridge = lax.psum(bridge_part, "gx").astype(jnp.bfloat16)
    tokens = talker_stream.shape[1]
    groups = HEADS // KVH
    scale = 1.0 / math.sqrt(HD)
    picks = (text_index[0][:, None] == jnp.arange(rows_seq, dtype=jnp.int32)[None, :]).astype(
        jnp.bfloat16
    )
    mixed = talker_stream[0].astype(jnp.float32) + jnp.dot(
        picks, bridge, preferred_element_type=jnp.float32
    )
    normal = (
        mixed * lax.rsqrt(jnp.mean(mixed * mixed, axis=1, keepdims=True) + norm_eps) * norm_gain
    ).astype(jnp.bfloat16)
    low_query = jnp.dot(normal, a_query, preferred_element_type=jnp.float32).astype(jnp.bfloat16)
    low_value = jnp.dot(normal, a_value, preferred_element_type=jnp.float32).astype(jnp.bfloat16)
    slab_rows = lax.all_gather(normal, "gy", axis=0, tiled=True)
    projected = jnp.concatenate(
        [
            jnp.dot(slab_rows, w_query, preferred_element_type=jnp.float32),
            jnp.dot(slab_rows, w_key, preferred_element_type=jnp.float32),
            jnp.dot(slab_rows, w_value, preferred_element_type=jnp.float32),
        ],
        axis=1,
    )
    returned = lax.all_to_all(projected, "gy", split_axis=0, concat_axis=1, tiled=True)
    parcels = returned.reshape(tokens, lax.axis_size("gy"), -1)
    query_cols = w_query.shape[1]
    key_cols = w_key.shape[1]
    base_query = parcels[:, :, :query_cols].reshape(tokens, -1)
    base_key = parcels[:, :, query_cols : query_cols + key_cols].reshape(tokens, -1)
    base_value = parcels[:, :, query_cols + key_cols :].reshape(tokens, -1)
    first_pos = lax.axis_index("gx") * tokens
    cosine, sine_table = angle_tables(first_pos, tokens)
    query_pre = base_query + jnp.dot(low_query, b_query, preferred_element_type=jnp.float32)
    query = rotate(query_pre.reshape(tokens, KVH, groups, HD), cosine, sine_table, 1.0).astype(
        jnp.bfloat16
    )
    key_local = (
        rotate(base_key.reshape(tokens, KVH, HD), cosine, sine_table, 1.0)
        .astype(jnp.bfloat16)
        .reshape(tokens, KVH * HD)
    )
    value_local = (
        base_value + jnp.dot(low_value, b_value, preferred_element_type=jnp.float32)
    ).astype(jnp.bfloat16)
    key_all, value_all = (
        lax.all_gather(key_local, "gx", axis=0, tiled=True),
        lax.all_gather(value_local, "gx", axis=0, tiled=True),
    )
    length = key_all.shape[0]
    key_rows = key_all.reshape(length, KVH, HD)
    value_rows = value_all.reshape(length, KVH, HD)
    query_places = first_pos + jnp.arange(tokens, dtype=jnp.int32)
    key_places = jnp.arange(length, dtype=jnp.int32)
    causal = (key_places[None, :] <= query_places[:, None]) | (key_places[None, :] < span_offset[0])
    scores = (
        jnp.einsum("tkgd,skd->kgts", query, key_rows, preferred_element_type=jnp.float32) * scale
    )
    scores = jnp.where(causal, scores, -1e30)
    row_max = jnp.max(scores, axis=-1, keepdims=True)
    weights = jnp.exp(scores - row_max)
    probs = (weights / jnp.sum(weights, axis=-1, keepdims=True)).astype(jnp.bfloat16)
    attended = jnp.einsum(
        "kgts,skd->tkgd", probs, value_rows, preferred_element_type=jnp.float32
    ).astype(jnp.bfloat16)
    grad_four = out_grad[0].reshape(tokens, KVH, groups, HD)
    inner_prod = jnp.sum(grad_four.astype(jnp.float32) * attended.astype(jnp.float32), axis=-1)
    dprob = jnp.einsum("tkgd,skd->kgts", grad_four, value_rows, preferred_element_type=jnp.float32)
    dscore = (
        probs.astype(jnp.float32) * (dprob - jnp.transpose(inner_prod, (1, 2, 0))[..., None])
    ).astype(jnp.bfloat16)
    dquery = (
        jnp.einsum("kgts,skd->tkgd", dscore, key_rows, preferred_element_type=jnp.float32) * scale
    )
    query_grad = (
        rotate(dquery, cosine, sine_table, -1.0).reshape(tokens, HEADS * HD).astype(jnp.bfloat16)
    )
    block = probs
    term = jnp.einsum("kgts,tkgd->skd", block, grad_four, preferred_element_type=jnp.float32)
    value_grad = sent_and_summed(
        term.reshape(tokens * lax.axis_size("gx"), KVH * HD), "gx", 0
    ).astype(jnp.bfloat16)
    part_bq = jnp.einsum("tr,tc->rc", low_query, query_grad, preferred_element_type=jnp.float32)
    part_bv = jnp.einsum("tr,tc->rc", low_value, value_grad, preferred_element_type=jnp.float32)
    dlow_query = jnp.einsum(
        "tc,rc->tr", query_grad, b_query, preferred_element_type=jnp.float32
    ).astype(jnp.bfloat16)
    dlow_value = jnp.einsum(
        "tc,rc->tr", value_grad, b_value, preferred_element_type=jnp.float32
    ).astype(jnp.bfloat16)
    part_aq = jnp.einsum("td,tr->dr", normal, dlow_query, preferred_element_type=jnp.float32)
    part_av = jnp.einsum("td,tr->dr", normal, dlow_value, preferred_element_type=jnp.float32)
    grad_aq, grad_bq, grad_av, grad_bv = lax.psum(
        (part_aq, part_bq, part_av, part_bv), ("gx", "gy")
    )
    attn_out = attended.reshape(1, tokens, HEADS * HD)
    return (attn_out, grad_aq, grad_bq, grad_av, grad_bv)


def solution(mesh):
    return jax.shard_map(
        on_device,
        mesh=mesh,
        in_specs=(
            P(None, None, "gx"),
            P("gy", None, "gx"),
            P("gx", "gy"),
            P("gx", "gy"),
            P("gy", "gx"),
            P("gx", None),
            P("gy", "gx", None),
            P(),
            P(None, "gy"),
            P(None, "gy"),
            P(None, "gy"),
            P(),
            P(),
            P(),
            P(),
            P("gy", "gx"),
            P("gy"),
            P("gy", "gx", None),
        ),
        out_specs=(P("gy", "gx", None), P(), P(), P(), P()),
        check_vma=False,
    )
```

profile of v0, /device:TPU:1, one launch (start us, length us, event | category | flops | bytes accessed | tf_op | source)
XLA Modules:
  0.0 656.1 jit_solution(4535558930171179902)
XLA Ops:
  7.2 3.4 fusion.59
  10.7 1.1 fusion.60
  11.8 2.1 pad_maximum_fusion
  13.9 5.3 copy.44
  19.2 52.4 %all_to_all.31 = f32[16,8,7392]{2,1,0:T(8,128)} all-to-all(f32[16,8,7392]{2,1,0:T(8,128)} %bitcast.99), channel_id=1, replica_groups=mesh['gx'=16,'gy'=8] {'gx'}, dimensions={0} | all-to-all | bytes 7569408 | tf_op jit(solution)/shard_map/all_to_all | solution.py:25
  71.6 2.3 reduce_sum.54
  74.0 21.7 %all_gather.12 = bf16[128,3696]{1,0:T(8,128)(2,1)S(1)} all-gather(bf16[8,3696]{1,0:T(8,128)(2,1)S(1)} %fusion.37), channel_id=1, replica_groups=mesh['gx'=16,'gy'=8] {'gx'}, dimensions={0}, use_global_device_ids=true | all-gather | bytes 1005312 | tf_op jit(solution)/shard_map/all_gather | solution.py:81
  95.7 2.8 fusion.61
  98.5 15.4 %all_to_all.32 = f32[8,16,512]{2,1,0:T(8,128)S(1)} all-to-all(f32[8,16,512]{2,1,0:T(8,128)S(1)} %bitcast.105), channel_id=1, replica_groups=mesh['gx'=16,'gy'=8] {'gy'}, dimensions={0} | all-to-all | bytes 524288 | tf_op jit(solution)/shard_map/all_to_all | solution.py:25
  114.0 2.7 fusion.46
  116.7 52.2 %all-reduce.5 = bf16[16,3584]{1,0:T(8,128)(2,1)S(1)} all-reduce(f32[16,3584]{1,0:T(8,128)S(1)} %fusion.46), channel_id=1, replica_groups=mesh['gx'=16,'gy'=8] {'gx'}, use_global_device_ids=true, to_apply=%region_2.3 | all-reduce | flops 57344 | bytes 344064 | tf_op jit(solution)/shard_map/psum | solution.py:88
  168.9 0.7 multiply_reduce_fusion
  169.6 1.4 multiply_convert_fusion
  171.1 128.6 %all-gather.4.cloned.1.call-done = bf16[1536,3584]{1,0:T(8,128)(2,1)} async-done(((bf16[192,3584]{1,0:T(8,128)(2,1)}), bf16[1536,3584]{1,0:T(8,128)(2,1)}) %all-gather.4.cloned.1.call-update) | async-done | bytes 11010064 | tf_op jit(solution)/shard_map/all_gather | solution.py:103
  299.7 7.2 %fusion.62 = f32[1536,224]{0,1:T(8,128)S(1)} fusion(bf16[1536,3584]{1,0:T(8,128)(2,1)} %all-gather.4.cloned.1.call-done, bf16[3584,224]{0,1:T(8,128)(2,1)S(1)} %copy-done), kind=kOutput, calls=%fused_computation.82 | convolution fusion | flops 2466250752 | bytes 13991936 | tf_op jit(solution)/shard_map/dot_general | solution.py:106
  307.0 3.3 fusion.63
  310.3 3.3 fusion.64
  313.7 2.1 all_to_all.23
  315.8 3.9 copy.45
  319.7 4.4 all-to-all-start.2
  324.2 0.4 broadcast_multiply_fusion
  324.8 29.3 %all-to-all-done.2 = f32[8,192,288]{1,2,0:T(8,128)} async-done(((f32[8,192,288]{1,2,0:T(8,128)}), f32[8,192,288]{1,2,0:T(8,128)}, u32[]{:S(2)}, u32[]{:S(2)}) %all-to-all-start.2) | async-done | bytes 1769504 | tf_op jit(solution)/shard_map/all_to_all | solution.py:112
  354.0 1.8 fusion.56
  355.9 0.7 copy.49
  357.6 1.7 reshape_squeeze.3
  359.3 1.3 fusion.14
  360.5 0.5 convolution_convert_fusion.2
  361.1 1.2 convolution_convert_fusion.3
  362.3 1.7 slice.50
  364.0 1.6 copy.73
  365.6 2.9 convolution_add_fusion.1
  368.5 1.7 reshape.214
  370.2 0.8 copy.46
  371.0 1.8 fusion.31
  372.8 0.5 fusion.57
  373.3 2.0 subtract_convert_fusion.1
  375.3 13.8 %all-gather.8.cloned.1.call-done = bf16[3072,256]{1,0:T(8,128)(2,1)} async-done(((bf16[192,256]{1,0:T(8,128)(2,1)}), bf16[3072,256]{1,0:T(8,128)(2,1)}) %all-gather.8.cloned.1.call-update) | async-done | bytes 1572880 | tf_op jit(solution)/shard_map/all_gather | solution.py:134
  389.1 1.7 copy.50
  390.8 19.7 %fusion.58 = (f32[2,7,192]{2,1,0:T(8,128)S(1)}, f32[2,7,192,3072]{3,2,1,0:T(8,128)}) fusion(bf16[3072,2,128,1]{0,2,3,1:T(8,128)(2,1)S(1)} %bitcast.103, pred[192,3072]{1,0:T(8,128)(4,1)} %fusion.14, bf16[192,2,7,64]{3,0,2,1:T(8,128)(2,1)} %get-tuple-element.10, bf16[192,2,7,64]{3,0,2,1:T(8,128)(2,1)} %get-tuple-element.9), kind=kOutput, calls=%fused_computation.78 | convolution fusion | flops 2148338688 | bytes 35891712 | tf_op jit(solution)/shard_map/sub | solution.py:148
  410.5 13.5 %divide_convert_fusion = bf16[2,7,192,3072]{3,2,1,0:T(8,128)(2,1)S(1)} fusion(f32[2,7,192,3072]{3,2,1,0:T(8,128)} %get-tuple-element.25, f32[2,7,192]{2,1,0:T(8,128)S(1)} %get-tuple-element.24), kind=kLoop, calls=%fused_computation.5 | loop fusion | flops 16515072 | bytes 49555968 | tf_op jit(solution)/shard_map/convert_element_type | solution.py:149
  424.1 8.7 %convolution_bitcast_fusion = f32[3072,2,128]{2,0,1:T(8,128)} fusion(bf16[2,7,192,3072]{3,2,1,0:T(8,128)(2,1)S(1)} %divide_convert_fusion, bf16[192,2,7,128]{3,2,1,0:T(8,128)(2,1)S(1)} %copy-done.6), kind=kOutput, calls=%fused_computation.16 | convolution fusion | flops 2113929216 | bytes 20348928 | tf_op jit(solution)/shard_map/kgts,tkgd->skd/dot_general | solution.py:166
  432.7 7.1 %copy.63 = f32[3072,2,128]{2,1,0:T(2,128)} copy(f32[3072,2,128]{2,0,1:T(8,128)} %convolution_bitcast_fusion) | data formatting | bytes 6291456 | tf_op jit(solution)/shard_map/kgts,tkgd->skd/transpose | solution.py:166
  439.9 5.5 reshape_reshape.7
  445.3 4.4 all-to-all-start.3
  449.9 2.5 reshape.211
  452.4 9.7 %multiply_reduce_fusion.1 = (f32[192,2,7]{0,2,1:T(8,128)S(1)}, bf16[192,2,7,128]{3,0,2,1:T(8,128)(2,1)}) fusion(bf16[192,2,7,128]{3,2,1,0:T(8,128)(2,1)} %reshape_squeeze.3, bf16[2,7,192,3072]{3,2,1,0:T(8,128)(2,1)} %copy-done.3, bf16[3072,2,128,1]{2,1,0,3:T(2,128)(2,1)S(1)} %bitcast.101), kind=kOutput, calls=%fused_computation.31 | convolution fusion | flops 2115646848 | bytes 19474944 | tf_op jit(solution)/shard_map/kgts,skd->tkgd/dot_general | solution.py:150
  462.1 14.0 %fusion.18 = f32[192,2,7,128]{3,0,2,1:T(8,128)} fusion(bf16[3072,2,128,1]{0,2,3,1:T(8,128)(2,1)} %bitcast.104, bf16[2,7,192,3072]{3,2,1,0:T(8,128)(2,1)} %copy-done.3, f32[2,7,192]{2,1,0:T(8,128)S(1)} %bitcast.111, bf16[3072,2,128,1]{2,1,0,3:T(2,128)(2,1)S(1)} %bitcast.102, bf16[192,2,7,128]{3,2,1,0:T(8,128)(2,1)} %reshape_squeeze.3), kind=kOutput, calls=%fused_computation.25 | convolution fusion | flops 4261232640 | bytes 21735936 | tf_op jit(solution)/shard_map/kgts,skd->tkgd/dot_general | solution.py:160
  476.0 2.4 subtract_convert_fusion
  478.8 0.5 copy.61
  479.3 0.7 convert_element_type.101
  480.0 1.0 fusion.65
  481.1 1.9 fusion.32
  482.9 5.2 all-to-all-done.3
  488.2 2.1 reduce_sum.59
  490.3 0.8 fusion.66
  491.1 1.5 fusion.33
  492.5 1.1 copy-done.7
  493.6 0.5 copy.56
  494.1 1.6 reshape.215
  495.7 149.1 %all-reduce.4.cloned.1.call-done = (f32[3584,64]{0,1:T(8,128)}, f32[64,1792]{1,0:T(8,128)}, f32[3584,64]{0,1:T(8,128)}, f32[64,256]{1,0:T(8,128)}) async-done(((f32[3584,64]{0,1:T(8,128)}, f32[64,1792]{1,0:T(8,128)}, f32[3584,64]{0,1:T(8,128)}, f32[64,256]{1,0:T(8,128)}), (f32[3584,64]{0,1:T(8,128)}, f32[64,1792]{1,0:T(8,128)}, f32[3584,64]{0,1:T(8,128)}, f32[64,256]{1,0:T(8,128)})) %all-reduce.4.cloned.1.call-update) | async-done | bytes 2359312 | tf_op jit(solution)/shard_map/psum | solution.py:180
  644.7 2.3 copy.108
  647.1 0.8 copy.109
  647.8 0.9 copy.110
  648.8 0.6 copy.111
  (79 shorter events, 1.6 us)
Async XLA Ops:
  7.2 292.5 %copy-start = (bf16[3584,224]{0,1:T(8,128)(2,1)S(1)}, bf16[3584,224]{0,1:T(8,128)(2,1)}, u32[]{:S(2)}) copy-start(bf16[3584,224]{0,1:T(8,128)(2,1)} %param.26) | copy-start | bytes 4816900
  7.2 292.5 %all-gather.4.cloned.1.call-start = ((), (), s32[]{:S(2)}) async-start(), calls=%async_computation.4 | async-start | bytes 12386304 | tf_op jit(solution)/shard_map/all_gather | solution.py:103
  7.2 3.5 copy-start.5
  7.2 3.5 copy-start.14
  95.7 18.2 %copy-start.26 = (bf16[1,16,512]{2,1,0:T(8,128)(2,1)S(1)}, bf16[1,16,512]{2,1,0:T(8,128)(2,1)}, u32[]{:S(2)}) copy-start(bf16[1,16,512]{2,1,0:T(8,128)(2,1)} %param.19) | copy-start | bytes 49156
  113.9 54.9 %copy-start.9 = (bf16[1,192,3584]{2,1,0:T(8,128)(2,1)S(1)}, bf16[1,192,3584]{2,1,0:T(8,128)(2,1)}, u32[]{:S(2)}) copy-start(bf16[1,192,3584]{2,1,0:T(8,128)(2,1)} %param.24) | copy-start | bytes 4128772
  114.0 54.9 %copy-start.28 = (s32[1,192]{1,0:T(1,128)S(1)}, s32[1,192]{1,0:T(1,128)}, u32[]{:S(2)}) copy-start(s32[1,192]{1,0:T(1,128)} %param.33) | copy-start | bytes 2308
  168.9 0.7 copy-start.27
  171.1 135.8 %copy-start.22 = (bf16[3584,32]{0,1:T(8,128)(2,1)S(1)}, bf16[3584,32]{0,1:T(8,128)(2,1)}, u32[]{:S(2)}) copy-start(bf16[3584,32]{0,1:T(8,128)(2,1)} %param.27) | copy-start | bytes 688132
  299.7 7.3 %copy-start.2 = (bf16[1536,3584]{1,0:T(8,128)(2,1)S(1)}, bf16[1536,3584]{1,0:T(8,128)(2,1)}, u32[]{:S(2)}) copy-start(bf16[1536,3584]{1,0:T(8,128)(2,1)} %all-gather.4.cloned.1.call-done) | copy-start | bytes 33030148
  307.0 3.3 copy-start.23
  319.7 34.3 %all-to-all-start.2 = ((f32[8,192,288]{1,2,0:T(8,128)}), f32[8,192,288]{1,2,0:T(8,128)}, u32[]{:S(2)}, u32[]{:S(2)}) async-start(f32[8,192,288]{1,2,0:T(8,128)} %copy.45), calls=%async_computation.2 | async-start | bytes 4718592 | tf_op jit(solution)/shard_map/all_to_all | solution.py:112
  324.1 33.5 %copy-start.13 = (bf16[1,192,1792]{2,1,0:T(8,128)(2,1)S(1)}, bf16[1,192,1792]{2,1,0:T(8,128)(2,1)}, u32[]{:S(2)}) copy-start(bf16[1,192,1792]{2,1,0:T(8,128)(2,1)} %param.35) | copy-start | bytes 2064388
  324.1 65.0 %all-gather.8.cloned.1.call-start = ((), (), s32[]{:S(2)}) async-start(), calls=%async_computation.6 | async-start | bytes 1671168 | tf_op jit(solution)/shard_map/all_gather | solution.py:134
  355.8 4.7 copy-start.4
  355.8 4.7 copy-start.15
  356.6 93.2 %all-gather.6.cloned.1.call-start = ((), (), s32[]{:S(2)}) async-start(), calls=%async_computation.5 | async-start | bytes 1671168 | tf_op jit(solution)/shard_map/all_gather | solution.py:135
  357.6 3.5 copy-start.16
  361.1 4.5 copy-start.18
  368.5 1.7 copy-start.10
  368.5 2.5 copy-start.20
  390.8 19.7 %copy-start.8 = (bf16[3072,256]{0,1:T(8,128)(2,1)}, bf16[3072,256]{0,1:T(8,128)(2,1)S(1)}, u32[]{:S(2)}) copy-start(bf16[3072,256]{0,1:T(8,128)(2,1)S(1)} %copy.50) | copy-start | bytes 4718596
  410.5 13.5 %copy-start.6 = (bf16[192,2,7,128]{3,2,1,0:T(8,128)(2,1)S(1)}, bf16[192,2,7,128]{3,2,1,0:T(8,128)(2,1)}, u32[]{:S(2)}) copy-start(bf16[192,2,7,128]{3,2,1,0:T(8,128)(2,1)} %reshape_squeeze.3) | copy-start | bytes 2064388
  424.0 8.7 %copy-start.3 = (bf16[2,7,192,3072]{3,2,1,0:T(8,128)(2,1)}, bf16[2,7,192,3072]{3,2,1,0:T(8,128)(2,1)S(1)}, u32[]{:S(2)}) copy-start(bf16[2,7,192,3072]{3,2,1,0:T(8,128)(2,1)S(1)} %divide_convert_fusion) | copy-start | bytes 49545220
  445.3 42.8 %all-to-all-start.3 = ((f32[16,192,256]{2,1,0:T(8,128)}), f32[16,192,256]{2,1,0:T(8,128)}, u32[]{:S(2)}, u32[]{:S(2)}) async-start(f32[16,192,256]{2,1,0:T(8,128)} %reshape_reshape.7), calls=%async_computation.3 | async-start | bytes 6291456 | tf_op jit(solution)/shard_map/all_to_all | solution.py:25
  449.8 194.9 %all-reduce.4.cloned.1.call-start = ((), (), s32[]{:S(2)}) async-start(), calls=%async_computation.7 | async-start | bytes 4718592 | tf_op jit(solution)/shard_map/psum | solution.py:180
  478.8 1.2 copy-start.19
  478.8 2.3 copy-start.11
  482.9 7.3 %copy-start.21 = (bf16[192,64]{0,1:T(8,128)(2,1)S(1)}, bf16[192,64]{0,1:T(8,128)(2,1)}, u32[]{:S(2)}) copy-start(bf16[192,64]{0,1:T(8,128)(2,1)} %convolution_convert_fusion.3) | copy-start | bytes 73732
  482.9 8.1 %copy-start.24 = (bf16[64,256]{1,0:T(8,128)(2,1)S(1)}, bf16[64,256]{1,0:T(8,128)(2,1)}, u32[]{:S(2)}) copy-start(bf16[64,256]{1,0:T(8,128)(2,1)} %param.32) | copy-start | bytes 98308
  492.5 1.1 copy-start.7
  644.7 2.3 copy-start.17
  644.7 3.1 copy-start.12
  644.7 4.7 copy-start.1
  647.1 1.7 copy-start.25
Sparse Core Ops, SparseCore 0:
  171.2 128.4 all-gather.3
  356.8 32.2 all-gather.7
  390.8 32.8 all-gather.5
  492.7 152.0 all-reduce.3
where the time goes:
time: 666 us; the launch traced here: 656 us
  waiting for transfers between devices  326 us (49%)
  blocking collectives  142 us (21%)
  matrix products  88.1 us (13%)
  local copies, waits for them, and re-layouts  47.9 us (7%)
  other arithmetic  28.1 us (4%)
  between operations  15.1 us (2%)
  starting transfers between devices  9.2 us (1%)
    psum x1, waiting for transfers between devices, on_device(): lax.psum((part_aq, part_bq, part_av, part_bv), ('gx', 'gy'))  149 us
    all_gather x1, waiting for transfers between devices, on_device(): slab_rows = lax.all_gather(normal, 'gy', axis=0, tiled=True)  129 us
    all_to_all x2, blocking collectives, sent_and_summed(): parts = lax.all_to_all(cut_along(array, dim, size), axis, 0, 0, tiled=True)  67.9 us
    psum x1, blocking collectives, on_device(): bridge = lax.psum(bridge_part, 'gx').astype(jnp.bfloat16)  52.2 us
    all_to_all x1, waiting for transfers between devices, on_device(): lax.all_to_all(projected, 'gy', split_axis=0, concat_axis=1, tiled=True)  29.3 us
    all_gather x1, blocking collectives, on_device(): lax.all_gather(hidden, 'gx', axis=0, tiled=True)  21.7 us
    sub x1, matrix products, on_device(): weights = jnp.exp(scores - row_max)  19.7 us
    dot_general x1, matrix products, on_device(): jnp.einsum('kgts,skd->tkgd', dscore, key_rows, preferred_element_type=jnp...  14 us
  transfers between devices with their start and end apart: 6, of which 5 were waited for; matrix products, arithmetic and copies ran while one was open for 17% of the time, Pallas kernels for 0%

commit v1 on v0

v1 whole, which is shorter than its diff:
```python
import functools
import math

import jax
import jax.numpy as jnp
from jax import lax
from jax.experimental import pallas as pl
from jax.experimental.pallas import tpu as pltpu
from jax.sharding import PartitionSpec as P

HEADS = 14
KVH = 2
HD = 128
MESH = pl.DeviceIdType.MESH
F32 = jnp.float32
BF16 = jnp.bfloat16

rope_base = 1000000.0
norm_eps = 1e-06


def angle_tables(first_pos, length):
    position = (first_pos + jnp.arange(length, dtype=jnp.int32)).astype(jnp.float32)
    frequency = rope_base ** (-(2.0 * jnp.arange(HD // 2, dtype=jnp.float32)) / HD)
    angles = position[:, None] * frequency[None, :]
    return (jnp.cos(angles), jnp.sin(angles))


def place():
    gx = lax.axis_index("gx")
    gy = lax.axis_index("gy")
    return gx, gy, gx // 2, gx % 2


def greet(peers):
    barrier = pltpu.get_barrier_semaphore()
    for peer in peers:
        pl.semaphore_signal(barrier, inc=1, device_id=peer, device_id_type=MESH)
    pl.semaphore_wait(barrier, len(peers))


def remote(src, dst, send_sem, recv_sem, peer):
    return pltpu.make_async_remote_copy(
        src_ref=src,
        dst_ref=dst,
        send_sem=send_sem,
        recv_sem=recv_sem,
        device_id=peer,
        device_id_type=MESH,
    )


def send(*args):
    copy = remote(*args)
    copy.start()
    return copy


def dot_nt(a, b):
    return lax.dot_general(a, b, (((1,), (1,)), ((), ())), preferred_element_type=F32)


HALF = 1920
REST = 1776
CHUNK = 640
GROUPS = (
    (768, (("aq", 3584), ("bq", 1792), ("bv", 256))),
    (512, (("av", 3584),)),
)


def segments(group):
    piece, parts = GROUPS[group]
    start = 0
    for name, width in parts:
        done = 0
        while done < width:
            chunk, offset = divmod(start + done, piece)
            size = min(width - done, piece - offset)
            yield name, done, chunk, offset, size
            done += size
        start += width
    if start < 8 * piece:
        chunk, offset = divmod(start, piece)
        while chunk < 8:
            yield None, 0, chunk, offset, piece - offset
            chunk, offset = chunk + 1, 0


class Box:
    pass


INPUTS = [
    "x", "resid", "gate", "up", "down", "bridge", "wq", "wk", "wv", "stream", "og", "a_q",
    "a_v", "b_q", "b_v", "gain", "index", "cos", "sin", "lim",
]
OUTPUTS = ["attn", "aq", "av", "bq", "bv"]


def dma(*shape):
    return pltpu.SemaphoreType.DMA(shape)


def shared_scratch():
    vmem = pltpu.VMEM
    table = dict(
        all_q=vmem((1792, 3584), BF16),
        all_kv=vmem((2, 256, 3584), BF16),
        x_v=vmem((128, 512), BF16),
        resid_v=vmem((16, 512), BF16),
        stream_v=vmem((192, 3584), BF16),
        og_v=vmem((192, 1792), BF16),
        a_v_q=vmem((64, 3584), BF16),
        a_v_v=vmem((64, 3584), BF16),
        b_v_q=vmem((64, 1792), BF16),
        b_v_v=vmem((64, 256), BF16),
        pair_tx=vmem((8, 16, 2 * HALF), BF16),
        pair_rx=vmem((8, 16, 2 * HALF), BF16),
        chip_tx=vmem((7, 16, 2 * HALF), BF16),
        chip_rx=vmem((7, 16, 2 * HALF), BF16),
        hidden=vmem((2, 8, 16, HALF), BF16),
        down_tx=vmem((8, 16, 512), BF16),
        down_rx=vmem((7, 16, 512), BF16),
        bridge_own=vmem((2, 16, 1792), F32),
        bridge_rx=vmem((16, 1792), F32),
        bridge_tx=vmem((16, 1792), BF16),
        bridge_peers=vmem((7, 16, 1792), BF16),
        bridge_half=vmem((2, 16, 1792), BF16),
        kv=vmem((8, 2, 192, 512), BF16),
        low=vmem((8, 2, 192, 128), BF16),
        dl_tx=vmem((16, 64, 192), BF16),
        dl_rx=vmem((15, 64, 192), BF16),
        load_sem=dma(18),
        pair_sem=dma(2),
        chip_sem=dma(2, 7),
        hid_sem=dma(2, 7),
        hidf_sem=dma(2, 8),
        gy_sem=dma(2, 7),
        bp_sem=dma(2),
        bc_sem=dma(2, 7),
        bf_sem=dma(2),
        wq_sem=dma(2, 16),
        wkv_sem=dma(2, 16),
        kv_sem=dma(2, 7),
        kvf_sem=dma(2, 8),
        low_sem=dma(2, 7),
        lowf_sem=dma(2, 8),
        dl_sem=dma(2, 15),
    )
    for n, (piece, _) in enumerate(GROUPS):
        table.update(
            {
                f"packed{n}": vmem((2, 8, 32, piece), BF16),
                f"g_pair{n}": vmem((8, 32, piece), BF16),
                f"g_tx{n}": vmem((7, 32, piece), BF16),
                f"g_rx{n}": vmem((7, 32, piece), BF16),
                f"y_tx{n}": vmem((8, 4, piece), F32),
                f"y_rx{n}": vmem((7, 4, piece), F32),
                f"y_all{n}": vmem((8, 4, piece), F32),
                f"g_all{n}": vmem((2, 8, 32, piece), BF16),
                f"gp_sem{n}": dma(2),
                f"gc_sem{n}": dma(2, 7),
                f"gy1_sem{n}": dma(2, 7),
                f"gy2_sem{n}": dma(2, 7),
                f"ga_sem{n}": dma(2, 7),
                f"gf_sem{n}": dma(2, 8),
            }
        )
    return table


THINKER = dict(
    gate_w=pltpu.VMEM((2, HALF, 512), BF16),
    up_w=pltpu.VMEM((2, HALF, 512), BF16),
    down_w=pltpu.VMEM((2, HALF, 512), BF16),
    bridge_w=pltpu.VMEM((512, 3584), BF16),
    own_half=pltpu.VMEM((8, 16, 2 * HALF), F32),
    down_own=pltpu.VMEM((8, 16, 512), F32),
)
TALKER = dict(
    mixed=pltpu.VMEM((192, 3584), F32),
    normal=pltpu.VMEM((192, 3584), BF16),
    query=pltpu.VMEM((HEADS, 192, HD), BF16),
    score=pltpu.VMEM((192, 3072), F32),
    expo=pltpu.VMEM((192, 3072), BF16),
    dvt=pltpu.VMEM((KVH, HD, 3072), F32),
    qgrad=pltpu.VMEM((192, 1792), BF16),
    p_aq=pltpu.VMEM((64, 3584), F32),
    p_av=pltpu.VMEM((64, 3584), F32),
    p_bq=pltpu.VMEM((64, 1792), F32),
    p_bv=pltpu.VMEM((64, 256), F32),
)


def weight_copy(r, kind, n):
    gx, gy, chip, core = place()
    z = gy // 2
    x_hi = gy % 2
    flip = 1 - x_hi
    up, down, far = (z + 1) % 4 * 2, (z + 3) % 4 * 2, (z + 2) % 4 * 2
    cross = ((chip + 1 - 2 * (chip % 2)) * 2 + core, z * 2 + flip)
    z_up, z_down = (gx, up + x_hi), (gx, down + x_hi)
    partner = (chip * 2 + 1 - core, gy)
    piece, part, peer = (
        (gy, None, cross),
        (gy, None, z_up),
        (gy, None, z_down),
        (z * 2 + flip, None, z_up),
        (z * 2 + flip, None, z_down),
        (down + x_hi, 0, z_up),
        (up + x_hi, 1, z_down),
        (down + flip, 0, z_up),
        (up + flip, 1, z_down),
        (z * 2 + flip, None, partner),
        (down + x_hi, None, partner),
        (up + x_hi, None, partner),
        (down + flip, None, partner),
        (up + flip, None, partner),
        (far + x_hi, None, partner),
        (far + flip, None, partner),
    )[n]
    cols = pl.ds(pl.multiple_of(core * 1792, 128), 1792)
    if kind == "q":
        rows = 224 if part is None else 112
        first = pl.multiple_of(piece * 224 + (0 if part is None else 112 * part), 16)
        ref, sem = r.all_q.at[pl.ds(first, rows), cols], r.wq_sem
    else:
        kinds = pl.ds(0, 2) if part is None else pl.ds(part, 1)
        rows = pl.ds(pl.multiple_of(piece * 32, 32), 32)
        ref, sem = r.all_kv.at[kinds, rows, cols], r.wkv_sem
    return remote(ref, ref, sem.at[0, n], sem.at[1, n], peer)


def weights_go(r, kind, *numbers):
    for n in numbers:
        weight_copy(r, kind, n).start()


def weights_wait(r, kind, *numbers):
    for n in numbers:
        weight_copy(r, kind, n).wait()


def early_loads(r):
    gy = lax.axis_index("gy")
    rows = pl.ds(pl.multiple_of(gy * 32, 32), 32)
    plan = [
        (r.wk, r.all_kv.at[0, rows]),
        (r.wv, r.all_kv.at[1, rows]),
        (r.wq, r.all_q.at[pl.ds(pl.multiple_of(gy * 224, 32), 224)]),
        (r.x, r.x_v),
        (r.resid, r.resid_v),
    ]
    return [pltpu.make_async_copy(a, b, r.load_sem.at[i]) for i, (a, b) in enumerate(plan)]


def late_loads(r):
    plan = [
        (r.stream, r.stream_v),
        (r.a_q, r.a_v_q),
        (r.a_v, r.a_v_v),
        (r.b_q, r.b_v_q),
        (r.b_v, r.b_v_v),
        (r.og, r.og_v),
    ]
    return [pltpu.make_async_copy(a, b, r.load_sem.at[5 + i]) for i, (a, b) in enumerate(plan)]


def think(r):
    gx, gy, chip, core = place()
    other = 1 - core
    partner = (chip * 2 + other, gy)
    chips = [((chip + k) % 8 * 2 + core, gy) for k in range(1, 8)]
    columns = [(gx, (gy + k) % 8) for k in range(1, 8)]
    row = [((gx + k) % 16, gy) for k in range(1, 16)]
    cross = ((chip + 1 - 2 * (chip % 2)) * 2 + core, gy + 1 - 2 * (gy % 2))

    first = early_loads(r)
    for copy in first:
        copy.start()
    plan = [
        (r.gate.at[pl.ds(0, HALF)], r.gate_w.at[0]),
        (r.gate.at[pl.ds(HALF, REST)], r.gate_w.at[1, pl.ds(0, REST)]),
        (r.up.at[pl.ds(0, HALF)], r.up_w.at[0]),
        (r.up.at[pl.ds(HALF, REST)], r.up_w.at[1, pl.ds(0, REST)]),
        (r.down.at[pl.ds(0, HALF)], r.down_w.at[0]),
        (r.down.at[pl.ds(HALF, REST)], r.down_w.at[1, pl.ds(0, REST)]),
        (r.bridge, r.bridge_w),
    ]
    loads = [pltpu.make_async_copy(a, b, r.load_sem.at[11 + i]) for i, (a, b) in enumerate(plan)]
    for copy in loads:
        copy.start()
    for copy in late_loads(r):
        copy.start()
    pad = jnp.zeros((HALF - REST, 512), BF16)
    r.gate_w[1, REST:] = pad
    r.up_w[1, REST:] = pad
    r.down_w[1, REST:] = pad

    greet(row + columns + [cross])

    first[0].wait()
    first[1].wait()
    weights_go(r, "kv", 0, 1, 2)
    first[2].wait()
    weights_go(r, "q", 0, 1, 2)

    first[3].wait()
    first[4].wait()
    for copy in loads[:4]:
        copy.wait()
    x = r.x_v[...]
    for half, is_own in ((other, False), (core, True)):
        for side, weight in ((0, r.gate_w), (1, r.up_w)):
            for c in range(HALF // CHUNK):
                part = dot_nt(x, weight[half, c * CHUNK : (c + 1) * CHUNK])
                part = part.reshape(8, 16, CHUNK)
                lo = side * HALF + c * CHUNK
                if is_own:
                    r.own_half[:, :, lo : lo + CHUNK] = part
                else:
                    r.pair_tx[:, :, lo : lo + CHUNK] = part.astype(BF16)
        if not is_own:
            pair_copy = send(r.pair_tx, r.pair_rx, r.pair_sem.at[0], r.pair_sem.at[1], partner)
    pair_copy.wait()

    chip_copies = []
    for k in range(1, 8):
        peer = (chip + k) % 8
        r.chip_tx[k - 1] = (r.own_half[peer] + r.pair_rx[peer].astype(F32)).astype(BF16)
        chip_copies.append(
            send(
                r.chip_tx.at[k - 1],
                r.chip_rx.at[k - 1],
                r.chip_sem.at[0, k - 1],
                r.chip_sem.at[1, k - 1],
                chips[k - 1],
            )
        )
    total = r.own_half[chip] + r.pair_rx[chip].astype(F32)
    for k in range(7):
        chip_copies[k].wait()
        total = total + r.chip_rx[k].astype(F32)
    gate = total[:, :HALF]
    r.hidden[core, chip] = (gate / (1.0 + jnp.exp(-gate)) * total[:, HALF:]).astype(BF16)

    fan_out(r.hidden, r.hid_sem, chip, core, chips)
    finish = relay_to_partner(r.hidden, r.hid_sem, r.hidf_sem, chip, core, chips, partner)
    loads[4].wait()
    loads[5].wait()
    finish()
    down = jnp.dot(r.hidden[0].reshape(128, HALF), r.down_w[0], preferred_element_type=F32)
    down = down + jnp.dot(
        r.hidden[1].reshape(128, HALF), r.down_w[1], preferred_element_type=F32
    )
    down = down.reshape(8, 16, 512)
    r.down_own[...] = down
    r.down_tx[...] = down.astype(BF16)
    gy_copies = [
        send(
            r.down_tx.at[(gy + k) % 8],
            r.down_rx.at[k - 1],
            r.gy_sem.at[0, k - 1],
            r.gy_sem.at[1, k - 1],
            columns[k - 1],
        )
        for k in range(1, 8)
    ]
    weights_wait(r, "kv", 0, 1, 2)
    weights_go(r, "kv", 3, 4, 5, 6, 9, 10, 11)
    loads[6].wait()
    tokens = r.down_own[gy] + r.resid_v[...].astype(F32)
    for k in range(7):
        gy_copies[k].wait()
        tokens = tokens + r.down_rx[k].astype(F32)
    weights_wait(r, "q", 0, 1, 2)
    weights_go(r, "q", 5, 6, 9, 10, 11)

    thinker_out = tokens.astype(BF16)
    for h in range(2):
        r.bridge_own[h] = jnp.dot(
            thinker_out, r.bridge_w[:, h * 1792 : (h + 1) * 1792], preferred_element_type=F32
        )
    send(r.bridge_own.at[other], r.bridge_rx, r.bp_sem.at[0], r.bp_sem.at[1], partner).wait()
    summed = r.bridge_own[core] + r.bridge_rx[...]
    r.bridge_tx[...] = summed.astype(BF16)
    b_copies = [
        send(r.bridge_tx, r.bridge_peers.at[k], r.bc_sem.at[0, k], r.bc_sem.at[1, k], chips[k])
        for k in range(7)
    ]
    weights_wait(r, "kv", 3, 4)
    weights_go(r, "kv", 7, 8, 12, 13)
    weights_go(r, "q", 3, 4)
    for k in range(7):
        b_copies[k].wait()
        summed = summed + r.bridge_peers[k].astype(F32)
    r.bridge_half[core] = summed.astype(BF16)
    send(
        r.bridge_half.at[core], r.bridge_half.at[core], r.bf_sem.at[0], r.bf_sem.at[1], partner
    ).wait()


def fan_out(ref, sem, chip, core, chips):
    here = ref.at[chip, core] if ref.shape[0] == 8 else ref.at[core, chip]
    for k in range(7):
        send(here, here, sem.at[0, k], sem.at[1, k], chips[k])


def relay_to_partner(ref, sem, fwd_sem, chip, core, chips, partner):
    def at(which):
        return ref.at[which, core] if ref.shape[0] == 8 else ref.at[core, which]

    here = at(chip)
    passed = [send(here, here, fwd_sem.at[0, 7], fwd_sem.at[1, 7], partner)]
    for k in range(7):
        remote(here, here, sem.at[0, k], sem.at[1, k], chips[k]).wait()
        block = at((chip + 7 - k) % 8)
        passed.append(send(block, block, fwd_sem.at[0, k], fwd_sem.at[1, k], partner))

    def finish():
        for copy in passed:
            copy.wait()

    return finish


def reduce_group(r, n, parts, outs):
    gx, gy, chip, core = place()
    other = 1 - core
    partner = (chip * 2 + other, gy)
    chips = [((chip + k) % 8 * 2 + core, gy) for k in range(1, 8)]
    columns = [(gx, (gy + k) % 8) for k in range(1, 8)]

    def own(name):
        return getattr(r, f"{name}{n}")

    packed, g_pair, g_tx, g_rx = own("packed"), own("g_pair"), own("g_tx"), own("g_rx")
    y_tx, y_rx, y_all, g_all = own("y_tx"), own("y_rx"), own("y_all"), own("g_all")
    for name, done, chunk, offset, size in segments(n):
        for h in range(2):
            if name is None:
                packed[h, chunk, :, offset : offset + size] = jnp.zeros((32, size), BF16)
            else:
                packed[h, chunk, :, offset : offset + size] = parts[name][
                    32 * h : 32 * h + 32, done : done + size
                ].astype(BF16)
    sem = own("gp_sem")
    pair = send(packed.at[other], g_pair, sem.at[0], sem.at[1], partner)
    yield
    pair.wait()
    sem = own("gc_sem")
    copies = []
    for k in range(1, 8):
        peer = (chip + k) % 8
        g_tx[k - 1] = (packed[core, peer].astype(F32) + g_pair[peer].astype(F32)).astype(BF16)
        copies.append(
            send(g_tx.at[k - 1], g_rx.at[k - 1], sem.at[0, k - 1], sem.at[1, k - 1], chips[k - 1])
        )
    total = packed[core, chip].astype(F32) + g_pair[chip].astype(F32)
    yield
    for k in range(7):
        copies[k].wait()
        total = total + g_rx[k].astype(F32)
    for i in range(8):
        y_tx[i] = total[4 * i : 4 * i + 4]
    sem = own("gy1_sem")
    copies = [
        send(
            y_tx.at[(gy + k) % 8], y_rx.at[k - 1], sem.at[0, k - 1], sem.at[1, k - 1], columns[k - 1]
        )
        for k in range(1, 8)
    ]
    total = y_tx[gy]
    yield
    for k in range(7):
        copies[k].wait()
        total = total + y_rx[k]
    y_all[gy] = total
    sem = own("gy2_sem")
    copies = [
        send(y_all.at[gy], y_all.at[gy], sem.at[0, k], sem.at[1, k], columns[k]) for k in range(7)
    ]
    yield
    for copy in copies:
        copy.wait()
    g_all[core, chip] = jnp.concatenate([y_all[i] for i in range(8)], axis=0).astype(BF16)
    fan_out(g_all, own("ga_sem"), chip, core, chips)
    yield
    finish = relay_to_partner(g_all, own("ga_sem"), own("gf_sem"), chip, core, chips, partner)
    yield
    finish()
    for name, done, chunk, offset, size in segments(n):
        if name is not None:
            for h in range(2):
                outs[name][32 * h : 32 * h + 32, done : done + size] = g_all[
                    h, chunk, :, offset : offset + size
                ].astype(F32)


def talk(r):
    gx, gy, chip, core = place()
    other = 1 - core
    partner = (chip * 2 + other, gy)
    chips = [((chip + k) % 8 * 2 + core, gy) for k in range(1, 8)]
    row = [((gx + k) % 16, gy) for k in range(1, 16)]
    kv = r.kv

    for copy in late_loads(r):
        copy.wait()
    picks = (r.index[...] == lax.broadcasted_iota(jnp.int32, (192, 16), 1)).astype(BF16)
    squares = jnp.zeros((192, HD), F32)
    for c in range(7):
        at = slice(512 * c, 512 * c + 512)
        pieces = []
        for lo, hi in ((512 * c, 512 * c + 256), (512 * c + 256, 512 * c + 512)):
            half, off = divmod(lo, 1792)
            pieces.append(r.bridge_half[half, :, off : off + 256])
        rows = jnp.concatenate(pieces, axis=1)
        mix = r.stream_v[:, at].astype(F32) + jnp.dot(picks, rows, preferred_element_type=F32)
        r.mixed[:, at] = mix
        for t in range(4):
            m = mix[:, t * HD : (t + 1) * HD]
            squares = squares + m * m
    rate = lax.rsqrt(jnp.sum(squares, axis=1, keepdims=True) / 3584.0 + norm_eps)
    for c in range(7):
        at = slice(512 * c, 512 * c + 512)
        r.normal[:, at] = (r.mixed[:, at] * rate * r.gain[:, at]).astype(BF16)

    normal = r.normal[...]
    low_q = dot_nt(normal, r.a_v_q[...]).astype(BF16)
    low_v = dot_nt(normal, r.a_v_v[...]).astype(BF16)
    r.low[chip, core, :, :64] = low_q
    r.low[chip, core, :, 64:] = low_v
    weights_wait(r, "kv", 5, 6)
    weights_go(r, "kv", 14)
    weights_wait(r, "kv", 7, 8)
    weights_go(r, "kv", 15)
    weights_wait(r, "kv", *range(9, 16))
    keys = dot_nt(normal, r.all_kv[0])
    values = dot_nt(normal, r.all_kv[1]) + jnp.dot(
        low_v, r.b_v_v[...], preferred_element_type=F32
    )
    for g in range(KVH):
        head = keys[:, g * HD : (g + 1) * HD]
        kv[chip, core, :, g * HD : (g + 1) * HD] = (
            head * r.cos[...] + pltpu.roll(head, 64, 1) * r.sin[...]
        ).astype(BF16)
    kv[chip, core, :, 256:] = values.astype(BF16)
    fan_out(kv, r.kv_sem, chip, core, chips)
    fan_out(r.low, r.low_sem, chip, core, chips)
    r.dvt[...] = jnp.zeros_like(r.dvt)

    weights_wait(r, "q", 5, 6)
    weights_go(r, "q", 14)
    weights_wait(r, "q", 3, 4)
    weights_go(r, "q", 7, 8, 12, 13)
    kv_finish = relay_to_partner(kv, r.kv_sem, r.kvf_sem, chip, core, chips, partner)
    weights_wait(r, "q", 7, 8)
    weights_go(r, "q", 15)
    low_finish = relay_to_partner(r.low, r.low_sem, r.lowf_sem, chip, core, chips, partner)
    weights_wait(r, "q", *range(9, 16))

    def project(i, carry):
        at = pl.ds(pl.multiple_of(i * 256, 128), 256)
        pre = dot_nt(r.normal[...], r.all_q[at]) + jnp.dot(
            r.low[chip, core, :, :64], r.b_v_q[:, at], preferred_element_type=F32
        )
        for t in range(2):
            head = pre[:, t * HD : (t + 1) * HD]
            r.query[2 * i + t] = (
                head * r.cos[...] + pltpu.roll(head, 64, 1) * r.sin[...]
            ).astype(BF16)
        return carry

    lax.fori_loop(0, 7, project, 0)
    kv_finish()

    scale = 1.0 / math.sqrt(HD)
    fold = scale * math.log2(math.e)
    span = 768

    def keys_at(group, j):
        at = pl.ds(pl.multiple_of(group * HD, 128), HD)
        return kv[2 * j : 2 * j + 2, :, :, at].reshape(span, HD)

    def values_at(group, j):
        at = pl.ds(pl.multiple_of(256 + group * HD, 128), HD)
        return kv[2 * j : 2 * j + 2, :, :, at].reshape(span, HD)

    def attend(h, carry):
        group = h // 7
        at = pl.ds(pl.multiple_of(h * HD, 128), HD)
        q = r.query[h]
        lim = r.lim[...]
        top = jnp.full((192, HD), -jnp.inf, F32)
        for j in range(4):
            s = dot_nt(q, keys_at(group, j))
            spot = lax.broadcasted_iota(jnp.int32, (192, span), 1) + j * span
            s = jnp.where(spot <= lim, s, -1e30)
            r.score[:, j * span : (j + 1) * span] = s
            for t in range(span // HD):
                top = jnp.maximum(top, s[:, t * HD : (t + 1) * HD])
        peak = jnp.max(top, axis=1, keepdims=True) * fold
        mass = jnp.zeros((192, HD), F32)
        out = jnp.zeros((192, HD), F32)
        for j in range(4):
            e = jnp.exp2(r.score[:, j * span : (j + 1) * span] * fold - peak)
            for t in range(span // HD):
                mass = mass + e[:, t * HD : (t + 1) * HD]
            e = e.astype(BF16)
            r.expo[:, j * span : (j + 1) * span] = e
            out = out + jnp.dot(e, values_at(group, j), preferred_element_type=F32)
        inverse = 1.0 / jnp.sum(mass, axis=1, keepdims=True)
        out = (out * inverse).astype(BF16)
        r.attn[:, at] = out
        cot = r.og_v[:, at]
        wide = cot.astype(F32)
        inner = jnp.sum(wide * out.astype(F32), axis=1, keepdims=True)
        turned = jnp.transpose(wide * inverse).astype(BF16)
        dq = jnp.zeros((192, HD), F32)
        for j in range(4):
            e = r.expo[:, j * span : (j + 1) * span]
            dp = dot_nt(cot, values_at(group, j))
            ds = (e.astype(F32) * (dp - inner)).astype(BF16)
            dq = dq + jnp.dot(ds, keys_at(group, j), preferred_element_type=F32)
            r.dvt[group, :, j * span : (j + 1) * span] += jnp.dot(
                turned, e, preferred_element_type=F32
            )
        dq = dq * (inverse * scale)
        r.qgrad[:, at] = (dq * r.cos[...] - pltpu.roll(dq, 64, 1) * r.sin[...]).astype(BF16)
        return carry

    lax.fori_loop(0, HEADS, attend, 0)

    for j in range(8):
        at = slice(384 * j, 384 * j + 384)
        part = jnp.dot(
            r.b_v_v[:, :HD], r.dvt[0, :, at].astype(BF16), preferred_element_type=F32
        ) + jnp.dot(r.b_v_v[:, HD:], r.dvt[1, :, at].astype(BF16), preferred_element_type=F32)
        r.dl_tx[2 * j] = part[:, :192].astype(BF16)
        r.dl_tx[2 * j + 1] = pltpu.roll(part, 192, 1)[:, :192].astype(BF16)
    dl_copies = [
        send(
            r.dl_tx.at[(gx + k) % 16],
            r.dl_rx.at[k - 1],
            r.dl_sem.at[0, k - 1],
            r.dl_sem.at[1, k - 1],
            row[k - 1],
        )
        for k in range(1, 16)
    ]
    low_finish()
    low_t = jnp.transpose(r.low[chip, core].astype(F32)).astype(BF16)
    r.p_bq[...] = jnp.dot(low_t[:64], r.qgrad[...], preferred_element_type=F32)
    dlow_q = dot_nt(r.b_v_q[...], r.qgrad[...]).astype(BF16)
    r.p_aq[...] = jnp.dot(dlow_q, r.normal[...], preferred_element_type=F32)
    for g in range(KVH):
        part = jnp.zeros((HD, HD), F32)
        for j in range(4):
            low = r.low[2 * j : 2 * j + 2].reshape(span, HD)
            part = part + jnp.dot(
                r.dvt[g, :, j * span : (j + 1) * span].astype(BF16),
                low,
                preferred_element_type=F32,
            )
        r.p_bv[:, g * HD : (g + 1) * HD] = jnp.transpose(part)[64:]
    parts = dict(aq=r.p_aq, av=r.p_av, bq=r.p_bq, bv=r.p_bv)
    outs = dict(aq=r.aq, av=r.av, bq=r.bq, bv=r.bv)
    early = reduce_group(r, 0, parts, outs)
    next(early)
    next(early)
    dlow = r.dl_tx[gx].astype(F32)
    for k in range(15):
        dl_copies[k].wait()
        dlow = dlow + r.dl_rx[k].astype(F32)
    r.p_av[...] = jnp.dot(dlow.astype(BF16), r.normal[...], preferred_element_type=F32)
    late = reduce_group(r, 1, parts, outs)
    running = [late, early]
    while running:
        for group in list(running):
            if next(group, "end") == "end":
                running.remove(group)


def kernel(names, *refs):
    r = Box()
    for name, ref in zip(names, refs, strict=True):
        setattr(r, name, ref)

    def scoped(run, table):
        def inner(*more):
            box = Box()
            box.__dict__.update(r.__dict__)
            for name, ref in zip(table, more, strict=True):
                setattr(box, name, ref)
            run(box)

        pl.run_scoped(inner, *table.values())

    scoped(think, THINKER)
    scoped(talk, TALKER)


def whole(*args):
    vmem = pl.BlockSpec(memory_space=pltpu.VMEM)
    hbm = pl.BlockSpec(memory_space=pltpu.HBM)
    scratch = shared_scratch()
    names = INPUTS + OUTPUTS + list(scratch)
    return pl.pallas_call(
        functools.partial(kernel, names),
        out_shape=(
            jax.ShapeDtypeStruct((192, 1792), BF16),
            jax.ShapeDtypeStruct((64, 3584), F32),
            jax.ShapeDtypeStruct((64, 3584), F32),
            jax.ShapeDtypeStruct((64, 1792), F32),
            jax.ShapeDtypeStruct((64, 256), F32),
        ),
        in_specs=[hbm] * 15 + [vmem] * 5,
        out_specs=(vmem,) * 5,
        scratch_shapes=list(scratch.values()),
        compiler_params=pltpu.CompilerParams(
            collective_id=0, has_side_effects=True, vmem_limit_bytes=63 << 20
        ),
        name="layer",
    )(*args)


def on_device(
    thinker_normed,
    thinker_resid,
    gate_weight,
    up_weight,
    down_weight,
    bridge_weight,
    talker_stream,
    norm_gain,
    w_query,
    w_key,
    w_value,
    a_query,
    b_query,
    a_value,
    b_value,
    text_index,
    span_offset,
    out_grad,
):
    seq_count, rows_seq, columns = thinker_normed.shape
    tokens = talker_stream.shape[1]
    first_pos = lax.axis_index("gx") * tokens
    cosine, sine = angle_tables(first_pos, tokens)
    places = first_pos + jnp.arange(tokens, dtype=jnp.int32)
    limit = jnp.maximum(places, span_offset[0] - 1)[:, None]
    attn_out, grad_aq, grad_av, grad_bq, grad_bv = whole(
        thinker_normed.reshape(seq_count * rows_seq, columns),
        thinker_resid[0],
        gate_weight.T,
        up_weight.T,
        down_weight,
        bridge_weight,
        w_query.T,
        w_key.T,
        w_value.T,
        talker_stream[0],
        out_grad[0],
        a_query.T,
        a_value.T,
        b_query,
        b_value,
        norm_gain[None],
        text_index[0][:, None],
        jnp.concatenate([cosine, cosine], axis=1),
        jnp.concatenate([-sine, sine], axis=1),
        limit,
    )
    return (attn_out[None], grad_aq.T, grad_bq, grad_av.T, grad_bv)


def solution(mesh):
    return jax.shard_map(
        on_device,
        mesh=mesh,
        in_specs=(
            P(None, None, "gx"),
            P("gy", None, "gx"),
            P("gx", "gy"),
            P("gx", "gy"),
            P("gy", "gx"),
            P("gx", None),
            P("gy", "gx", None),
            P(),
            P(None, "gy"),
            P(None, "gy"),
            P(None, "gy"),
            P(),
            P(),
            P(),
            P(),
            P("gy", "gx"),
            P("gy"),
            P("gy", "gx", None),
        ),
        out_specs=(P("gy", "gx", None), P(), P(), P(), P()),
        check_vma=False,
    )
```

time: 666 us -> 184 us (0.28); the launches traced: 656 us -> 184 us
  waiting for transfers between devices: 326 us -> 0 us
  Pallas kernels: 0 us -> 170 us
  blocking collectives: 142 us -> 0 us
  matrix products: 88.1 us -> 0 us
  local copies, waits for them, and re-layouts: 47.9 us -> 10.4 us
  other arithmetic: 28.1 us -> 1.89 us
  between operations: 15.1 us -> 1.33 us
  starting transfers between devices: 9.2 us -> 0 us
    pallas_call x0 -> x1, Pallas kernels: none -> 170 us  [whole(): pl.pallas_call(functools.partial(kernel, names), out_shape=(jax.ShapeDtyp...]
    psum x1 -> x0, waiting for transfers between devices: 149 us -> none  [on_device(): lax.psum((part_aq, part_bq, part_av, part_bv), ('gx', 'gy'))]
    all_gather x3 -> x0, waiting for transfers between devices: 142 us -> none  [the longest x1 129 us: on_device(): slab_rows = lax.all_gather(normal, 'gy', axis=0, tiled=True)]
    dot_general x19 -> x0, matrix products: 68.4 us -> none  [the longest x1 14 us: on_device(): jnp.einsum('kgts,skd->tkgd', dscore, key_rows, preferred_element_type=jnp...]
    all_to_all x2 -> x0, blocking collectives: 67.9 us -> none  [sent_and_summed(): parts = lax.all_to_all(cut_along(array, dim, size), axis, 0, 0, tiled=True)]
    psum x1 -> x0, blocking collectives: 52.2 us -> none  [on_device(): bridge = lax.psum(bridge_part, 'gx').astype(jnp.bfloat16)]
    all_to_all x2 -> x0, waiting for transfers between devices: 34.5 us -> none  [the longest x1 29.3 us: on_device(): lax.all_to_all(projected, 'gy', split_axis=0, concat_axis=1, tiled=True)]
    all_gather x1 -> x0, blocking collectives: 21.7 us -> none  [on_device(): lax.all_gather(hidden, 'gx', axis=0, tiled=True)]
  transfers between devices with their start and end apart: 6 -> 0, of which waited for: 5 -> 0; matrix products, arithmetic and copies ran while one was open for 17% -> 0% of each run, Pallas kernels for 0% -> 0%
where the time goes in v1:
time: 184 us
  Pallas kernels  170 us (92%)
  local copies, waits for them, and re-layouts  10.4 us (6%)
  other arithmetic  1.89 us (1%)
    pallas_call x1, Pallas kernels, whole(): pl.pallas_call(functools.partial(kernel, names), out_shape=(jax.ShapeDtyp...  170 us
    unnamed x9, local copies, waits for them, and re-layouts  7.61 us

profile of v1, /device:TPU:1, one launch (start us, length us, event | category | flops | bytes accessed | tf_op | source)
XLA Modules:
  0.0 184.1 jit_solution(13092605239597447181)
XLA Ops:
  1.3 1.3 broadcast_in_dim.4.refs_15_
  2.6 0.7 add_maximum_fusion.refs_19_
  3.3 1.4 copy.23.refs_16_
  4.7 0.4 fusion
  5.2 0.8 pad_maximum_fusion
  6.0 170.5 %layer.1 = (bf16[192,1792]{1,0:T(8,128)(2,1)}, f32[64,3584]{1,0:T(8,128)}, f32[64,3584]{1,0:T(8,128)}, f32[64,1792]{1,0:T(8,128)}, f32[64,256]{1,0:T(8,128)}) custom-call(bf16[128,512]{1,0:T(8,128)(2,1)} %bitcast.28, bf16[16,512]{1,0:T(8,128)(2,1)} %bitcast.29, bf16[3696,512]{1,0:T(8,128)(2,1)} %bitcast.16, bf16[3696,512]{1,0:T(8,128)(2,1)} %bitcast.17, ...), custom_call_target="tpu_custom_call" | custom-call | tf_op jit(solution)/shard_map/layer/pallas_call | solution.py:710
  176.5 0.0 copy-start
  176.5 0.0 copy-start.1
  176.5 2.1 %copy.30 = bf16[1,192,1792]{2,1,0:T(8,128)(2,1)} copy(bf16[1,192,1792]{2,1,0:T(8,128)(2,1)} %bitcast.23) | data formatting | bytes 1376256
  178.6 2.2 %copy.31 = f32[3584,64]{0,1:T(8,128)} copy(f32[3584,64]{0,1:T(8,128)} %bitcast.21) | data formatting | bytes 1835008
  180.7 1.8 copy.32
  182.5 0.0 copy-done
  182.5 0.9 copy.33
  183.5 0.0 copy-done.1
  183.5 0.6 copy.34
  (2 shorter events, 0.0 us)
Async XLA Ops:
  176.5 6.1 %copy-start = (f32[64,3584]{1,0:T(8,128)S(1)}, f32[64,3584]{1,0:T(8,128)}, u32[]{:S(2)}) copy-start(f32[64,3584]{1,0:T(8,128)} %get-tuple-element.13) | copy-start | bytes 2752516
  176.5 7.0 %copy-start.1 = (f32[64,256]{1,0:T(8,128)S(1)}, f32[64,256]{1,0:T(8,128)}, u32[]{:S(2)}) copy-start(f32[64,256]{1,0:T(8,128)} %get-tuple-element.29) | copy-start | bytes 196612

commit v2 on v1

--- a/solution.py
+++ b/solution.py
@@ -3,6 +3,7 @@
 
 import jax
 import jax.numpy as jnp
+import numpy as np
 from jax import lax
 from jax.experimental import pallas as pl
 from jax.experimental.pallas import tpu as pltpu
@@ -17,13 +18,6 @@
 
 rope_base = 1000000.0
 norm_eps = 1e-06
-
-
-def angle_tables(first_pos, length):
-    position = (first_pos + jnp.arange(length, dtype=jnp.int32)).astype(jnp.float32)
-    frequency = rope_base ** (-(2.0 * jnp.arange(HD // 2, dtype=jnp.float32)) / HD)
-    angles = position[:, None] * frequency[None, :]
-    return (jnp.cos(angles), jnp.sin(angles))
 
 
 def place():
@@ -93,7 +87,7 @@
 
 INPUTS = [
     "x", "resid", "gate", "up", "down", "bridge", "wq", "wk", "wv", "stream", "og", "a_q",
-    "a_v", "b_q", "b_v", "gain", "index", "cos", "sin", "lim",
+    "a_v", "b_q", "b_v", "gain", "index", "freq", "offset",
 ]
 OUTPUTS = ["attn", "aq", "av", "bq", "bv"]
 
@@ -107,6 +101,8 @@
     table = dict(
         all_q=vmem((1792, 3584), BF16),
         all_kv=vmem((2, 256, 3584), BF16),
+        cos=vmem((192, 128), F32),
+        sin=vmem((192, 128), F32),
         x_v=vmem((128, 512), BF16),
         resid_v=vmem((16, 512), BF16),
         stream_v=vmem((192, 3584), BF16),
@@ -140,13 +136,14 @@
         bp_sem=dma(2),
         bc_sem=dma(2, 7),
         bf_sem=dma(2),
-        wq_sem=dma(2, 16),
+        wq_sem=dma(2, 18),
         wkv_sem=dma(2, 16),
         kv_sem=dma(2, 7),
         kvf_sem=dma(2, 8),
         low_sem=dma(2, 7),
         lowf_sem=dma(2, 8),
         dl_sem=dma(2, 15),
+        out_sem=dma(5),
     )
     for n, (piece, _) in enumerate(GROUPS):
         table.update(
@@ -182,8 +179,9 @@
     mixed=pltpu.VMEM((192, 3584), F32),
     normal=pltpu.VMEM((192, 3584), BF16),
     query=pltpu.VMEM((HEADS, 192, HD), BF16),
-    score=pltpu.VMEM((192, 3072), F32),
-    expo=pltpu.VMEM((192, 3072), BF16),
+    score=pltpu.VMEM((336, 3072), F32),
+    expo=pltpu.VMEM((336, 3072), BF16),
+    attn_v=pltpu.VMEM((192, 1792), BF16),
     dvt=pltpu.VMEM((KVH, HD, 3072), F32),
     qgrad=pltpu.VMEM((192, 1792), BF16),
     p_aq=pltpu.VMEM((64, 3584), F32),
@@ -206,8 +204,8 @@
         (gy, None, cross),
         (gy, None, z_up),
         (gy, None, z_down),
-        (z * 2 + flip, None, z_up),
-        (z * 2 + flip, None, z_down),
+        (z * 2 + flip, 0 if kind == "q" else None, z_up),
+        (z * 2 + flip, 1 if kind == "q" else None, z_down),
         (down + x_hi, 0, z_up),
         (up + x_hi, 1, z_down),
         (down + flip, 0, z_up),
@@ -219,6 +217,8 @@
         (up + flip, None, partner),
         (far + x_hi, None, partner),
         (far + flip, None, partner),
+        (down + x_hi, 1, cross),
+        (up + x_hi, 0, cross),
     )[n]
     cols = pl.ds(pl.multiple_of(core * 1792, 128), 1792)
     if kind == "q":
@@ -346,6 +346,11 @@
     r.hidden[core, chip] = (gate / (1.0 + jnp.exp(-gate)) * total[:, HALF:]).astype(BF16)
 
     fan_out(r.hidden, r.hid_sem, chip, core, chips)
+    place_at = gx * 192 + lax.broadcasted_iota(jnp.int32, (192, 128), 0)
+    angles = place_at.astype(F32) * r.freq[...]
+    r.cos[...] = jnp.cos(angles)
+    low_half = lax.broadcasted_iota(jnp.int32, (192, 128), 1) < 64
+    r.sin[...] = jnp.sin(angles) * jnp.where(low_half, -1.0, 1.0)
     finish = relay_to_partner(r.hidden, r.hid_sem, r.hidf_sem, chip, core, chips, partner)
     loads[4].wait()
     loads[5].wait()
@@ -375,7 +380,7 @@
         gy_copies[k].wait()
         tokens = tokens + r.down_rx[k].astype(F32)
     weights_wait(r, "q", 0, 1, 2)
-    weights_go(r, "q", 5, 6, 9, 10, 11)
+    weights_go(r, "q", 5, 6, 16, 17, 9, 10, 11)
 
     thinker_out = tokens.astype(BF16)
     for h in range(2):
@@ -508,7 +513,8 @@
 
     for copy in late_loads(r):
         copy.wait()
-    picks = (r.index[...] == lax.broadcasted_iota(jnp.int32, (192, 16), 1)).astype(BF16)
+    picks = (r.index[...] == lax.broadcasted_iota(jnp.int32, (16, 192), 0)).astype(F32)
+    picks = jnp.transpose(picks).astype(BF16)
     squares = jnp.zeros((192, HD), F32)
     for c in range(7):
         at = slice(512 * c, 512 * c + 512)
@@ -523,9 +529,9 @@
             m = mix[:, t * HD : (t + 1) * HD]
             squares = squares + m * m
     rate = lax.rsqrt(jnp.sum(squares, axis=1, keepdims=True) / 3584.0 + norm_eps)
-    for c in range(7):
-        at = slice(512 * c, 512 * c + 512)
-        r.normal[:, at] = (r.mixed[:, at] * rate * r.gain[:, at]).astype(BF16)
+    for c in range(28):
+        at = slice(128 * c, 128 * c + 128)
+        r.normal[:, at] = (r.mixed[:, at] * rate * r.gain[c : c + 1]).astype(BF16)
 
     normal = r.normal[...]
     low_q = dot_nt(normal, r.a_v_q[...]).astype(BF16)
@@ -554,11 +560,11 @@
     weights_wait(r, "q", 5, 6)
     weights_go(r, "q", 14)
     weights_wait(r, "q", 3, 4)
-    weights_go(r, "q", 7, 8, 12, 13)
-    kv_finish = relay_to_partner(kv, r.kv_sem, r.kvf_sem, chip, core, chips, partner)
+    weights_go(r, "q", 7, 8)
+    weights_wait(r, "q", 16, 17)
+    weights_go(r, "q", 12, 13)
     weights_wait(r, "q", 7, 8)
     weights_go(r, "q", 15)
-    low_finish = relay_to_partner(r.low, r.low_sem, r.lowf_sem, chip, core, chips, partner)
     weights_wait(r, "q", *range(9, 16))
 
     def project(i, carry):
@@ -574,6 +580,8 @@
         return carry
 
     lax.fori_loop(0, 7, project, 0)
+    kv_finish = relay_to_partner(kv, r.kv_sem, r.kvf_sem, chip, core, chips, partner)
+    low_finish = relay_to_partner(r.low, r.low_sem, r.lowf_sem, chip, core, chips, partner)
     kv_finish()
 
     scale = 1.0 / math.sqrt(HD)
@@ -588,22 +596,31 @@
         at = pl.ds(pl.multiple_of(256 + group * HD, 128), HD)
         return kv[2 * j : 2 * j + 2, :, :, at].reshape(span, HD)
 
-    def attend(h, carry):
-        group = h // 7
-        at = pl.ds(pl.multiple_of(h * HD, 128), HD)
-        q = r.query[h]
-        lim = r.lim[...]
-        top = jnp.full((192, HD), -jnp.inf, F32)
+    block, rows = 48, 336
+
+    def attend(b, carry):
+        group = b // 4
+        here = pl.ds(pl.multiple_of(b % 4 * block, 16), block)
+        heads = [pl.ds(pl.multiple_of((group * 7 + i) * HD, 128), HD) for i in range(7)]
+
+        def stacked(pieces):
+            return jnp.concatenate(pieces, axis=0)
+
+        q = r.query[pl.ds(group * 7, 7), here].reshape(rows, HD)
+        first = gx * 192 + b % 4 * block
+        place_at = first + lax.broadcasted_iota(jnp.int32, (block, 1), 0)
+        lim = stacked([jnp.maximum(place_at, r.offset[0] - 1)] * 7)
+        top = jnp.full((rows, HD), -jnp.inf, F32)
         for j in range(4):
             s = dot_nt(q, keys_at(group, j))
-            spot = lax.broadcasted_iota(jnp.int32, (192, span), 1) + j * span
+            spot = lax.broadcasted_iota(jnp.int32, (rows, span), 1) + j * span
             s = jnp.where(spot <= lim, s, -1e30)
             r.score[:, j * span : (j + 1) * span] = s
             for t in range(span // HD):
                 top = jnp.maximum(top, s[:, t * HD : (t + 1) * HD])
         peak = jnp.max(top, axis=1, keepdims=True) * fold
-        mass = jnp.zeros((192, HD), F32)
-        out = jnp.zeros((192, HD), F32)
+        mass = jnp.zeros((rows, HD), F32)
+        out = jnp.zeros((rows, HD), F32)
         for j in range(4):
             e = jnp.exp2(r.score[:, j * span : (j + 1) * span] * fold - peak)
             for t in range(span // HD):
@@ -613,12 +630,11 @@
             out = out + jnp.dot(e, values_at(group, j), preferred_element_type=F32)
         inverse = 1.0 / jnp.sum(mass, axis=1, keepdims=True)
         out = (out * inverse).astype(BF16)
-        r.attn[:, at] = out
-        cot = r.og_v[:, at]
+        cot = stacked([r.og_v[here, at] for at in heads])
         wide = cot.astype(F32)
         inner = jnp.sum(wide * out.astype(F32), axis=1, keepdims=True)
         turned = jnp.transpose(wide * inverse).astype(BF16)
-        dq = jnp.zeros((192, HD), F32)
+        dq = jnp.zeros((rows, HD), F32)
         for j in range(4):
             e = r.expo[:, j * span : (j + 1) * span]
             dp = dot_nt(cot, values_at(group, j))
@@ -628,10 +644,18 @@
                 turned, e, preferred_element_type=F32
             )
         dq = dq * (inverse * scale)
-        r.qgrad[:, at] = (dq * r.cos[...] - pltpu.roll(dq, 64, 1) * r.sin[...]).astype(BF16)
+        for i, at in enumerate(heads):
+            part = slice(block * i, block * i + block)
+            r.attn_v[here, at] = out[part]
+            piece = dq[part]
+            r.qgrad[here, at] = (
+                piece * r.cos[here] - pltpu.roll(piece, 64, 1) * r.sin[here]
+            ).astype(BF16)
         return carry
 
-    lax.fori_loop(0, HEADS, attend, 0)
+    lax.fori_loop(0, 2 * 4, attend, 0)
+    leaving = [pltpu.make_async_copy(r.attn_v, r.attn, r.out_sem.at[0])]
+    leaving[0].start()
 
     for j in range(8):
         at = slice(384 * j, 384 * j + 384)
@@ -666,7 +690,7 @@
             )
         r.p_bv[:, g * HD : (g + 1) * HD] = jnp.transpose(part)[64:]
     parts = dict(aq=r.p_aq, av=r.p_av, bq=r.p_bq, bv=r.p_bv)
-    outs = dict(aq=r.aq, av=r.av, bq=r.bq, bv=r.bv)
+    outs = parts
     early = reduce_group(r, 0, parts, outs)
     next(early)
     next(early)
@@ -681,6 +705,15 @@
         for group in list(running):
             if next(group, "end") == "end":
                 running.remove(group)
+                done = ("av",) if group is late else ("aq", "bq", "bv")
+                for name in done:
+                    copy = pltpu.make_async_copy(
+                        parts[name], getattr(r, name), r.out_sem.at[len(leaving)]
+                    )
+                    copy.start()
+                    leaving.append(copy)
+    for copy in leaving:
+        copy.wait()
 
 
 def kernel(names, *refs):
@@ -716,8 +749,8 @@
             jax.ShapeDtypeStruct((64, 1792), F32),
             jax.ShapeDtypeStruct((64, 256), F32),
         ),
-        in_specs=[hbm] * 15 + [vmem] * 5,
-        out_specs=(vmem,) * 5,
+        in_specs=[hbm] * 15 + [vmem] * 3 + [pl.BlockSpec(memory_space=pltpu.SMEM)],
+        out_specs=(hbm,) * 5,
         scratch_shapes=list(scratch.values()),
         compiler_params=pltpu.CompilerParams(
             collective_id=0, has_side_effects=True, vmem_limit_bytes=63 << 20
@@ -747,11 +780,7 @@
     out_grad,
 ):
     seq_count, rows_seq, columns = thinker_normed.shape
-    tokens = talker_stream.shape[1]
-    first_pos = lax.axis_index("gx") * tokens
-    cosine, sine = angle_tables(first_pos, tokens)
-    places = first_pos + jnp.arange(tokens, dtype=jnp.int32)
-    limit = jnp.maximum(places, span_offset[0] - 1)[:, None]
+    angle = np.float32(rope_base) ** (-(2.0 * np.arange(HD // 2, dtype=np.float32)) / HD)
     attn_out, grad_aq, grad_av, grad_bq, grad_bv = whole(
         thinker_normed.reshape(seq_count * rows_seq, columns),
         thinker_resid[0],
@@ -768,11 +797,10 @@
         a_value.T,
         b_query,
         b_value,
-        norm_gain[None],
-        text_index[0][:, None],
-        jnp.concatenate([cosine, cosine], axis=1),
-        jnp.concatenate([-sine, sine], axis=1),
-        limit,
+        norm_gain.reshape(28, 128),
+        text_index,
+        jnp.asarray(np.concatenate([angle, angle])[None], F32),
+        span_offset,
     )
     return (attn_out[None], grad_aq.T, grad_bq, grad_av.T, grad_bv)
 

time: 184 us -> 173 us (0.940)
  Pallas kernels: 170 us -> 164 us
  local copies, waits for them, and re-layouts: 10.4 us -> 7.61 us
  other arithmetic: 1.89 us -> 0 us
    pallas_call x1, Pallas kernels: 170 us -> 164 us  [whole(): pl.pallas_call(functools.partial(kernel, names), out_shape=(jax.ShapeDtyp...]
where the time goes in v2:
time: 173 us
  Pallas kernels  164 us (95%)
  local copies, waits for them, and re-layouts  7.61 us (4%)
    pallas_call x1, Pallas kernels, whole(): pl.pallas_call(functools.partial(kernel, names), out_shape=(jax.ShapeDtyp...  164 us
    unnamed x9, local copies, waits for them, and re-layouts  7.61 us

profile of v2, /device:TPU:1, one launch (start us, length us, event | category | flops | bytes accessed | tf_op | source)
XLA Modules:
  0.0 172.7 jit_solution(10708803033582314880)
XLA Ops:
  1.3 163.8 %layer.1 = (bf16[192,1792]{1,0:T(8,128)(2,1)}, f32[64,3584]{1,0:T(8,128)}, f32[64,3584]{1,0:T(8,128)}, f32[64,1792]{1,0:T(8,128)}, f32[64,256]{1,0:T(8,128)}) custom-call(bf16[128,512]{1,0:T(8,128)(2,1)} %bitcast.27, bf16[16,512]{1,0:T(8,128)(2,1)} %bitcast.28, bf16[3696,512]{1,0:T(8,128)(2,1)} %bitcast.15, bf16[3696,512]{1,0:T(8,128)(2,1)} %bitcast.16, ...), custom_call_target="tpu_custom_call" | custom-call | tf_op jit(solution)/shard_map/layer/pallas_call | solution.py:743
  165.1 0.0 copy-start
  165.1 0.0 copy-start.1
  165.1 2.1 %copy.30 = bf16[1,192,1792]{2,1,0:T(8,128)(2,1)} copy(bf16[1,192,1792]{2,1,0:T(8,128)(2,1)} %bitcast.22) | data formatting | bytes 1376256
  167.2 2.2 %copy.31 = f32[3584,64]{0,1:T(8,128)} copy(f32[3584,64]{0,1:T(8,128)} %bitcast.20) | data formatting | bytes 1835008
  169.4 1.8 %copy.32 = f32[64,1792]{1,0:T(8,128)} copy(f32[64,1792]{1,0:T(8,128)} %get-tuple-element.22) | data formatting | bytes 917504
  171.2 0.0 copy-done
  171.2 0.9 copy.33
  172.1 0.0 copy-done.1
  172.1 0.6 copy.34
Async XLA Ops:
  165.1 6.1 %copy-start = (f32[64,3584]{1,0:T(8,128)S(1)}, f32[64,3584]{1,0:T(8,128)}, u32[]{:S(2)}) copy-start(f32[64,3584]{1,0:T(8,128)} %get-tuple-element.13) | copy-start | bytes 2752516
  165.1 7.0 %copy-start.1 = (f32[64,256]{1,0:T(8,128)S(1)}, f32[64,256]{1,0:T(8,128)}, u32[]{:S(2)}) copy-start(f32[64,256]{1,0:T(8,128)} %get-tuple-element.24) | copy-start | bytes 196612

commit v3 on v2

--- a/solution.py
+++ b/solution.py
@@ -125,8 +125,10 @@
         bridge_half=vmem((2, 16, 1792), BF16),
         kv=vmem((8, 2, 192, 512), BF16),
         low=vmem((8, 2, 192, 128), BF16),
-        dl_tx=vmem((16, 64, 192), BF16),
-        dl_rx=vmem((15, 64, 192), BF16),
+        normal=vmem((2, 192, 3584), BF16),
+        dl_tx=vmem((16, 32, 384), BF16),
+        dl_rx=vmem((15, 32, 384), BF16),
+        norm_sem=dma(2),
         load_sem=dma(18),
         pair_sem=dma(2),
         chip_sem=dma(2, 7),
@@ -177,17 +179,21 @@
 )
 TALKER = dict(
     mixed=pltpu.VMEM((192, 3584), F32),
-    normal=pltpu.VMEM((192, 3584), BF16),
     query=pltpu.VMEM((HEADS, 192, HD), BF16),
     score=pltpu.VMEM((336, 3072), F32),
+    bias=pltpu.VMEM((48, 3072), F32),
     expo=pltpu.VMEM((336, 3072), BF16),
     attn_v=pltpu.VMEM((192, 1792), BF16),
     dvt=pltpu.VMEM((KVH, HD, 3072), F32),
     qgrad=pltpu.VMEM((192, 1792), BF16),
     p_aq=pltpu.VMEM((64, 3584), F32),
-    p_av=pltpu.VMEM((64, 3584), F32),
+    p_av=pltpu.VMEM((32, 3584), F32),
     p_bq=pltpu.VMEM((64, 1792), F32),
     p_bv=pltpu.VMEM((64, 256), F32),
+    o_aq=pltpu.VMEM((64, 3584), BF16),
+    o_av=pltpu.VMEM((64, 3584), BF16),
+    o_bq=pltpu.VMEM((64, 1792), BF16),
+    o_bv=pltpu.VMEM((64, 256), BF16),
 )
 
 
@@ -442,7 +448,12 @@
 
     packed, g_pair, g_tx, g_rx = own("packed"), own("g_pair"), own("g_tx"), own("g_rx")
     y_tx, y_rx, y_all, g_all = own("y_tx"), own("y_rx"), own("y_all"), own("g_all")
+    paired = n == 0
     for name, done, chunk, offset, size in segments(n):
+        if not paired:
+            value = jnp.zeros((32, size), F32) if name is None else parts[name][:, done : done + size]
+            packed[core, chunk, :, offset : offset + size] = value.astype(BF16)
+            continue
         for h in range(2):
             if name is None:
                 packed[h, chunk, :, offset : offset + size] = jnp.zeros((32, size), BF16)
@@ -450,19 +461,25 @@
                 packed[h, chunk, :, offset : offset + size] = parts[name][
                     32 * h : 32 * h + 32, done : done + size
                 ].astype(BF16)
-    sem = own("gp_sem")
-    pair = send(packed.at[other], g_pair, sem.at[0], sem.at[1], partner)
-    yield
-    pair.wait()
+    if paired:
+        sem = own("gp_sem")
+        pair = send(packed.at[other], g_pair, sem.at[0], sem.at[1], partner)
+        yield
+        pair.wait()
     sem = own("gc_sem")
     copies = []
     for k in range(1, 8):
         peer = (chip + k) % 8
-        g_tx[k - 1] = (packed[core, peer].astype(F32) + g_pair[peer].astype(F32)).astype(BF16)
+        block = packed.at[core, peer]
+        if paired:
+            block = g_tx.at[k - 1]
+            block[...] = (packed[core, peer].astype(F32) + g_pair[peer].astype(F32)).astype(BF16)
         copies.append(
-            send(g_tx.at[k - 1], g_rx.at[k - 1], sem.at[0, k - 1], sem.at[1, k - 1], chips[k - 1])
+            send(block, g_rx.at[k - 1], sem.at[0, k - 1], sem.at[1, k - 1], chips[k - 1])
         )
-    total = packed[core, chip].astype(F32) + g_pair[chip].astype(F32)
+    total = packed[core, chip].astype(F32)
+    if paired:
+        total = total + g_pair[chip].astype(F32)
     yield
     for k in range(7):
         copies[k].wait()
@@ -500,7 +517,7 @@
             for h in range(2):
                 outs[name][32 * h : 32 * h + 32, done : done + size] = g_all[
                     h, chunk, :, offset : offset + size
-                ].astype(F32)
+                ]
 
 
 def talk(r):
@@ -531,9 +548,9 @@
     rate = lax.rsqrt(jnp.sum(squares, axis=1, keepdims=True) / 3584.0 + norm_eps)
     for c in range(28):
         at = slice(128 * c, 128 * c + 128)
-        r.normal[:, at] = (r.mixed[:, at] * rate * r.gain[c : c + 1]).astype(BF16)
-
-    normal = r.normal[...]
+        r.normal[core, :, at] = (r.mixed[:, at] * rate * r.gain[c : c + 1]).astype(BF16)
+
+    normal = r.normal[core]
     low_q = dot_nt(normal, r.a_v_q[...]).astype(BF16)
     low_v = dot_nt(normal, r.a_v_v[...]).astype(BF16)
     r.low[chip, core, :, :64] = low_q
@@ -555,6 +572,8 @@
     kv[chip, core, :, 256:] = values.astype(BF16)
     fan_out(kv, r.kv_sem, chip, core, chips)
     fan_out(r.low, r.low_sem, chip, core, chips)
+    here = r.normal.at[core]
+    norm_copy = send(here, here, r.norm_sem.at[0], r.norm_sem.at[1], partner)
     r.dvt[...] = jnp.zeros_like(r.dvt)
 
     weights_wait(r, "q", 5, 6)
@@ -567,16 +586,18 @@
     weights_go(r, "q", 15)
     weights_wait(r, "q", *range(9, 16))
 
+    scale = 1.0 / math.sqrt(HD)
+    fold = scale * math.log2(math.e)
+
     def project(i, carry):
         at = pl.ds(pl.multiple_of(i * 256, 128), 256)
-        pre = dot_nt(r.normal[...], r.all_q[at]) + jnp.dot(
+        pre = dot_nt(r.normal[core], r.all_q[at]) + jnp.dot(
             r.low[chip, core, :, :64], r.b_v_q[:, at], preferred_element_type=F32
         )
         for t in range(2):
             head = pre[:, t * HD : (t + 1) * HD]
-            r.query[2 * i + t] = (
-                head * r.cos[...] + pltpu.roll(head, 64, 1) * r.sin[...]
-            ).astype(BF16)
+            turned = head * r.cos[...] + pltpu.roll(head, 64, 1) * r.sin[...]
+            r.query[2 * i + t] = (turned * fold).astype(BF16)
         return carry
 
     lax.fori_loop(0, 7, project, 0)
@@ -584,8 +605,6 @@
     low_finish = relay_to_partner(r.low, r.low_sem, r.lowf_sem, chip, core, chips, partner)
     kv_finish()
 
-    scale = 1.0 / math.sqrt(HD)
-    fold = scale * math.log2(math.e)
     span = 768
 
     def keys_at(group, j):
@@ -609,20 +628,22 @@
         q = r.query[pl.ds(group * 7, 7), here].reshape(rows, HD)
         first = gx * 192 + b % 4 * block
         place_at = first + lax.broadcasted_iota(jnp.int32, (block, 1), 0)
-        lim = stacked([jnp.maximum(place_at, r.offset[0] - 1)] * 7)
+        lim = jnp.maximum(place_at, r.offset[0] - 1)
+        for j in range(4):
+            spot = lax.broadcasted_iota(jnp.int32, (block, span), 1) + j * span
+            r.bias[:, j * span : (j + 1) * span] = jnp.where(spot <= lim, 0.0, -1e30)
         top = jnp.full((rows, HD), -jnp.inf, F32)
         for j in range(4):
-            s = dot_nt(q, keys_at(group, j))
-            spot = lax.broadcasted_iota(jnp.int32, (rows, span), 1) + j * span
-            s = jnp.where(spot <= lim, s, -1e30)
+            s = dot_nt(q, keys_at(group, j)).reshape(7, block, span)
+            s = (s + r.bias[:, j * span : (j + 1) * span][None]).reshape(rows, span)
             r.score[:, j * span : (j + 1) * span] = s
             for t in range(span // HD):
                 top = jnp.maximum(top, s[:, t * HD : (t + 1) * HD])
-        peak = jnp.max(top, axis=1, keepdims=True) * fold
+        peak = jnp.max(top, axis=1, keepdims=True)
         mass = jnp.zeros((rows, HD), F32)
         out = jnp.zeros((rows, HD), F32)
         for j in range(4):
-            e = jnp.exp2(r.score[:, j * span : (j + 1) * span] * fold - peak)
+            e = jnp.exp2(r.score[:, j * span : (j + 1) * span] - peak)
             for t in range(span // HD):
                 mass = mass + e[:, t * HD : (t + 1) * HD]
             e = e.astype(BF16)
@@ -637,8 +658,7 @@
         dq = jnp.zeros((rows, HD), F32)
         for j in range(4):
             e = r.expo[:, j * span : (j + 1) * span]
-            dp = dot_nt(cot, values_at(group, j))
-            ds = (e.astype(F32) * (dp - inner)).astype(BF16)
+            ds = (dot_nt(cot, values_at(group, j)) - inner).astype(BF16) * e
             dq = dq + jnp.dot(ds, keys_at(group, j), preferred_element_type=F32)
             r.dvt[group, :, j * span : (j + 1) * span] += jnp.dot(
                 turned, e, preferred_element_type=F32
@@ -662,8 +682,8 @@
         part = jnp.dot(
             r.b_v_v[:, :HD], r.dvt[0, :, at].astype(BF16), preferred_element_type=F32
         ) + jnp.dot(r.b_v_v[:, HD:], r.dvt[1, :, at].astype(BF16), preferred_element_type=F32)
-        r.dl_tx[2 * j] = part[:, :192].astype(BF16)
-        r.dl_tx[2 * j + 1] = pltpu.roll(part, 192, 1)[:, :192].astype(BF16)
+        r.dl_tx[2 * j] = part[:32].astype(BF16)
+        r.dl_tx[2 * j + 1] = part[32:].astype(BF16)
     dl_copies = [
         send(
             r.dl_tx.at[(gx + k) % 16],
@@ -678,7 +698,7 @@
     low_t = jnp.transpose(r.low[chip, core].astype(F32)).astype(BF16)
     r.p_bq[...] = jnp.dot(low_t[:64], r.qgrad[...], preferred_element_type=F32)
     dlow_q = dot_nt(r.b_v_q[...], r.qgrad[...]).astype(BF16)
-    r.p_aq[...] = jnp.dot(dlow_q, r.normal[...], preferred_element_type=F32)
+    r.p_aq[...] = jnp.dot(dlow_q, r.normal[core], preferred_element_type=F32)
     for g in range(KVH):
         part = jnp.zeros((HD, HD), F32)
         for j in range(4):
@@ -690,7 +710,7 @@
             )
         r.p_bv[:, g * HD : (g + 1) * HD] = jnp.transpose(part)[64:]
     parts = dict(aq=r.p_aq, av=r.p_av, bq=r.p_bq, bv=r.p_bv)
-    outs = parts
+    outs = dict(aq=r.o_aq, av=r.o_av, bq=r.o_bq, bv=r.o_bv)
     early = reduce_group(r, 0, parts, outs)
     next(early)
     next(early)
@@ -698,7 +718,9 @@
     for k in range(15):
         dl_copies[k].wait()
         dlow = dlow + r.dl_rx[k].astype(F32)
-    r.p_av[...] = jnp.dot(dlow.astype(BF16), r.normal[...], preferred_element_type=F32)
+    norm_copy.wait()
+    both = r.normal[...].reshape(384, 3584)
+    r.p_av[...] = jnp.dot(dlow.astype(BF16), both, preferred_element_type=F32)
     late = reduce_group(r, 1, parts, outs)
     running = [late, early]
     while running:
@@ -708,7 +730,7 @@
                 done = ("av",) if group is late else ("aq", "bq", "bv")
                 for name in done:
                     copy = pltpu.make_async_copy(
-                        parts[name], getattr(r, name), r.out_sem.at[len(leaving)]
+                        outs[name], getattr(r, name), r.out_sem.at[len(leaving)]
                     )
                     copy.start()
                     leaving.append(copy)
@@ -744,10 +766,10 @@
         functools.partial(kernel, names),
         out_shape=(
             jax.ShapeDtypeStruct((192, 1792), BF16),
-            jax.ShapeDtypeStruct((64, 3584), F32),
-            jax.ShapeDtypeStruct((64, 3584), F32),
-            jax.ShapeDtypeStruct((64, 1792), F32),
-            jax.ShapeDtypeStruct((64, 256), F32),
+            jax.ShapeDtypeStruct((64, 3584), BF16),
+            jax.ShapeDtypeStruct((64, 3584), BF16),
+            jax.ShapeDtypeStruct((64, 1792), BF16),
+            jax.ShapeDtypeStruct((64, 256), BF16),
         ),
         in_specs=[hbm] * 15 + [vmem] * 3 + [pl.BlockSpec(memory_space=pltpu.SMEM)],
         out_specs=(hbm,) * 5,
@@ -802,7 +824,13 @@
         jnp.asarray(np.concatenate([angle, angle])[None], F32),
         span_offset,
     )
-    return (attn_out[None], grad_aq.T, grad_bq, grad_av.T, grad_bv)
+    return (
+        attn_out[None],
+        grad_aq.astype(F32).T,
+        grad_bq.astype(F32),
+        grad_av.astype(F32).T,
+        grad_bv.astype(F32),
+    )
 
 
 def solution(mesh):

time: 173 us -> 166 us (0.960)
  local copies, waits for them, and re-layouts: 7.61 us -> 0.85 us
  Pallas kernels: 164 us -> 158 us
  other arithmetic: 0 us -> 5.76 us
    unnamed x9 -> x3, local copies, waits for them, and re-layouts: 7.61 us -> 0.85 us
    pallas_call x1, Pallas kernels: 164 us -> 158 us  [whole(): pl.pallas_call(functools.partial(kernel, names), out_shape=(jax.ShapeDtyp...]
    convert_element_type x0 -> x2, other arithmetic: none -> 3.13 us  [the longest x1 1.74 us: on_device(): grad_bq.astype(F32)]
    transpose x0 -> x1, other arithmetic: none -> 2.63 us  [on_device(): grad_av.astype(F32)]
where the time goes in v3:
time: 166 us; the launch traced here: 165 us
  Pallas kernels  158 us (95%)
  other arithmetic  5.76 us (3%)
    pallas_call x1, Pallas kernels, whole(): pl.pallas_call(functools.partial(kernel, names), out_shape=(jax.ShapeDtyp...  158 us

profile of v3, /device:TPU:1, one launch (start us, length us, event | category | flops | bytes accessed | tf_op | source)
XLA Modules:
  0.0 165.5 jit_solution(18129493188631581934)
XLA Ops:
  1.3 157.6 %layer.1 = (bf16[192,1792]{1,0:T(8,128)(2,1)}, bf16[64,3584]{1,0:T(8,128)(2,1)}, bf16[64,3584]{1,0:T(8,128)(2,1)}, bf16[64,1792]{1,0:T(8,128)(2,1)}, bf16[64,256]{1,0:T(8,128)(2,1)}) custom-call(bf16[128,512]{1,0:T(8,128)(2,1)} %bitcast.27, bf16[16,512]{1,0:T(8,128)(2,1)} %bitcast.28, bf16[3696,512]{1,0:T(8,128)(2,1)} %bitcast.17, ...), custom_call_target="tpu_custom_call" | custom-call | tf_op jit(solution)/shard_map/layer/pallas_call | solution.py:765
  158.9 0.0 copy-start
  158.9 2.6 %convert_bitcast_fusion = (f32[3584,64]{0,1:T(8,128)}, f32[3584,64]{0,1:T(8,128)}) fusion(bf16[64,3584]{1,0:T(8,128)(2,1)} %get-tuple-element.13, bf16[64,3584]{1,0:T(8,128)(2,1)} %get-tuple-element.11), kind=kLoop, calls=%fused_computation | loop fusion | flops 458752 | bytes 2752512 | tf_op jit(solution)/shard_map/transpose | solution.py:831
  161.5 1.7 %convert_element_type.8 = f32[64,1792]{1,0:T(8,128)} convert(bf16[64,1792]{1,0:T(8,128)(2,1)} %get-tuple-element.12) | non-fusion elementwise | flops 114688 | bytes 688128 | tf_op jit(solution)/shard_map/convert_element_type | solution.py:830
  163.2 1.4 convert_element_type.9
  164.6 0.0 copy-done
  164.6 0.8 copy.26
Async XLA Ops:
  158.9 5.8 %copy-start = (bf16[192,1792]{1,0:T(8,128)(2,1)S(1)}, bf16[192,1792]{1,0:T(8,128)(2,1)}, u32[]{:S(2)}) copy-start(bf16[192,1792]{1,0:T(8,128)(2,1)} %get-tuple-element.10) | copy-start | bytes 2064388
